TPU v7x, 32 devices: a whole 2x2x4 slice. The times are simulated.
32 devices in a mesh: dp: 2 (over x), yax: 4 (over z), xax: 4 (over y, core).
Axes of the slice: x: 2, y: 2, z: 4, core: 2. Of those that a mesh axis runs over, the one named last changes fastest.
Arguments:
- hidden: bfloat16 [128, 2048], P('dp', 'xax'), parts along dimension 0
- cache_len: int32 [128], P('dp'), parts along dimension 0
- k_cache: bfloat16 [128, 8192, 256], P(('dp', 'yax', 'xax')), parts along dimension 0
- v_cache: bfloat16 [128, 8192, 256], P(('dp', 'yax', 'xax')), parts along dimension 0
- g_attn: float32 [2048], P('xax')
- w_query: bfloat16 [2048, 2048], P('xax', 'yax')
- w_key: bfloat16 [2048, 256], P('xax')
- w_value: bfloat16 [2048, 256], P('xax')
- w_gate: bfloat16 [2048, 8192], P('xax', 'yax')
- w_up: bfloat16 [2048, 8192], P('xax', 'yax')
- w_out: bfloat16 [2048, 2048], P('yax', 'xax')
- w_down: bfloat16 [8192, 2048], P('yax', 'xax')
- g_final: float32 [2048], P('xax')
- embedding: bfloat16 [50304, 2048], P('yax', 'xax')
Outputs:
- output 1: bfloat16 [128, 256], P(('dp', 'yax', 'xax')), parts along dimension 0
- output 2: bfloat16 [128, 256], P(('dp', 'yax', 'xax')), parts along dimension 0
- output 3: float32 [128, 50304], P('dp', ('yax', 'xax')), parts along dimension 0
- output 4: float32 [128], P('dp'), parts along dimension 0
There are 2 independent parts. A program takes and returns all parts, laid end to end along the dimension named above; an argument that names none is the same for every part.
All inputs are finite; a program needn't handle non-finite values.
Results may differ from a plain program's by a relative error of at most 0.001.
Values are sent between devices in bfloat16 or wider.
A program may use at most 1 GiB of HBM per device.

v0:
```python
import jax
import jax.numpy as jnp
from jax import lax
from jax.sharding import PartitionSpec as P

EPS = 1e-6
ROPE_BASE = 10000.0


def rope_angle(positions, head_dim):
    half_dim = head_dim // 2
    inv_freq = ROPE_BASE ** (-(jnp.arange(half_dim, dtype=jnp.float32) * 2.0) / head_dim)
    return positions.astype(jnp.float32)[:, None] * inv_freq[None, :]


def rotary(values_in, angles):
    half_dim = values_in.shape[-1] // 2
    cos_a = jnp.cos(angles)
    sin_a = jnp.sin(angles)
    first = values_in[..., :half_dim]
    second = values_in[..., half_dim:]
    return jnp.concatenate([first * cos_a - second * sin_a, second * cos_a + first * sin_a], axis=-1)


def sharded_norm(values_in, gain, width):
    stats = jnp.stack([jnp.sum(values_in, axis=-1), jnp.sum(values_in * values_in, axis=-1)])
    stats = lax.psum(stats, "xax")
    row_mean = stats[0] / width
    row_var = stats[1] / width - row_mean * row_mean
    return (values_in - row_mean[:, None]) * lax.rsqrt(row_var + EPS)[:, None] * gain


def attend_local(query, k_cache, v_cache, key_new, value_new, lengths):
    score_scale = query.shape[-1] ** -0.5
    scores = jnp.einsum("bhe,bse->bhs", query, k_cache, preferred_element_type=jnp.float32) * score_scale
    score_new = jnp.einsum("bhe,be->bh", query, key_new, preferred_element_type=jnp.float32) * score_scale
    valid = jnp.arange(k_cache.shape[1])[None, None, :] < lengths[:, None, None]
    row_max = jnp.maximum(jnp.max(jnp.where(valid, scores, -jnp.inf), axis=-1), score_new)
    weights = jnp.where(valid, jnp.exp(scores - row_max[..., None]), 0.0)
    weight_new = jnp.exp(score_new - row_max)
    denominator = jnp.sum(weights, axis=-1) + weight_new
    prob_all = (weights / denominator[..., None]).astype(jnp.bfloat16)
    prob_new = (weight_new / denominator).astype(jnp.bfloat16)
    attn_out = jnp.einsum("bhs,bse->bhe", prob_all, v_cache, preferred_element_type=jnp.float32)
    attn_out = attn_out + prob_new.astype(jnp.float32)[..., None] * value_new.astype(jnp.float32)[:, None, :]
    return attn_out.astype(jnp.bfloat16)


def solution(mesh):
    y_size = mesh.shape["yax"]
    x_size = mesh.shape["xax"]
    row_spec = P(("dp", "yax", "xax"))

    def local_step(hidden, cache_len, k_cache, v_cache, g_attn, w_query, w_key, w_value,
                   w_gate, w_up, w_out, w_down, g_final, embedding):
        rows = hidden.shape[0]
        width = hidden.shape[1] * x_size
        own_rows = k_cache.shape[0]
        head_dim = k_cache.shape[2]
        q_cols = w_query.shape[1]
        kv_end = q_cols + 2 * head_dim
        ff_end = kv_end + w_gate.shape[1]
        y_idx = lax.axis_index("yax")
        x_idx = lax.axis_index("xax")
        own_start = (y_idx * x_size + x_idx) * own_rows

        residual = hidden.astype(jnp.float32)
        normed = sharded_norm(residual, g_attn, width).astype(jnp.bfloat16)
        proj_part = jnp.concatenate([
            jnp.dot(normed, w_query, preferred_element_type=jnp.float32),
            jnp.dot(normed, w_key, preferred_element_type=jnp.float32),
            jnp.dot(normed, w_value, preferred_element_type=jnp.float32),
            jnp.dot(normed, w_gate, preferred_element_type=jnp.float32),
            jnp.dot(normed, w_up, preferred_element_type=jnp.float32)], axis=1)
        projected = lax.psum(proj_part, "xax").astype(jnp.bfloat16)
        angles = rope_angle(cache_len, head_dim)
        query = projected[:, :q_cols].astype(jnp.float32).reshape(rows, q_cols // head_dim, head_dim)
        query = rotary(query, angles[:, None, :]).astype(jnp.bfloat16)
        key_new = rotary(projected[:, q_cols:q_cols + head_dim].astype(jnp.float32), angles).astype(jnp.bfloat16)
        value_new = projected[:, q_cols + head_dim:kv_end]
        gate = projected[:, kv_end:ff_end]
        up_val = projected[:, ff_end:]

        query_grp = lax.all_to_all(query, "yax", 0, 1, tiled=True)
        query_own = lax.dynamic_slice_in_dim(query_grp, x_idx * own_rows, own_rows, axis=0)
        key_own = lax.dynamic_slice_in_dim(key_new, own_start, own_rows, axis=0)
        value_own = lax.dynamic_slice_in_dim(value_new, own_start, own_rows, axis=0)
        len_own = lax.dynamic_slice_in_dim(cache_len, own_start, own_rows, axis=0)
        attn_own = attend_local(query_own, k_cache, v_cache, key_own, value_own, len_own)
        attn_grp = lax.all_gather(attn_own, "xax", axis=0, tiled=True)
        attn_heads = lax.all_to_all(attn_grp, "yax", 1, 0, tiled=True).reshape(rows, q_cols)

        mlp_act = (jax.nn.silu(gate.astype(jnp.float32)) * up_val.astype(jnp.float32)).astype(jnp.bfloat16)
        branch_sum = (jnp.dot(attn_heads, w_out, preferred_element_type=jnp.float32)
                      + jnp.dot(mlp_act, w_down, preferred_element_type=jnp.float32))
        residual_out = residual + lax.psum(branch_sum, "yax")
        final_norm = sharded_norm(residual_out, g_final, width).astype(jnp.bfloat16)
        logit_part = jnp.einsum("bd,vd->bv", final_norm, embedding, preferred_element_type=jnp.float32)
        logits = lax.psum_scatter(logit_part, "xax", scatter_dimension=1, tiled=True)
        row_max = lax.pmax(jnp.max(logits, axis=1), ("yax", "xax"))
        sum_exp = lax.psum(jnp.sum(jnp.exp(logits - row_max[:, None]), axis=1), ("yax", "xax"))
        log_norm = row_max + jnp.log(sum_exp)
        return key_own, value_own, logits - log_norm[:, None], log_norm

    in_specs = (P("dp", "xax"), P("dp"), row_spec, row_spec, P("xax"), P("xax", "yax"),
                P("xax", None), P("xax", None), P("xax", "yax"), P("xax", "yax"),
                P("yax", "xax"), P("yax", "xax"), P("xax"), P("yax", "xax"))
    out_specs = (row_spec, row_spec, P("dp", ("yax", "xax")), P("dp"))
    return jax.shard_map(local_step, mesh=mesh, in_specs=in_specs, out_specs=out_specs, check_vma=False)
```

profile of v0, /device:TPU:0, one launch (start us, length us, event | category | flops | bytes accessed | tf_op | source)
XLA Modules:
  0.0 293.2 jit_solution(15645539081061757824)
XLA Ops:
  7.2 0.0 copy-start
  7.2 1.1 convert_reduce_fusion
  8.3 8.4 %psum.35 = f32[2,64]{1,0:T(2,128)S(1)} all-reduce(f32[2,64]{1,0:T(2,128)S(1)} %pad_maximum_fusion.1), channel_id=1, replica_groups=mesh['dp'=2,'yax'=4,'xax'=4] {'xax'}, use_global_device_ids=true, to_apply=%region_2.0 | all-reduce | flops 128 | bytes 1024 | tf_op jit(solution)/shard_map/psum | solution.py:27
  16.8 0.0 copy-start.1
  16.8 0.0 copy-start.2
  16.8 0.0 copy-start.4
  16.8 1.5 convolution_dynamic-update-slice_fusion.2
  18.3 1.2 convolution_dynamic-update-slice_fusion.4
  19.5 1.2 convolution_dynamic-update-slice_fusion.3
  20.7 0.0 copy-done
  20.7 1.4 convolution_dynamic-update-slice_fusion.1
  22.1 0.0 copy-done.1
  22.1 0.0 copy-done.2
  22.1 0.0 copy-done.4
  22.1 0.0 copy-start.9
  22.2 0.5 convolution_dynamic-update-slice_fusion
  22.7 27.8 %all-reduce.8 = bf16[64,5120]{1,0:T(8,128)(2,1)} all-reduce(f32[64,5120]{1,0:T(8,128)S(1)} %convolution_dynamic-update-slice_fusion), channel_id=1, replica_groups=mesh['dp'=2,'yax'=4,'xax'=4] {'xax'}, use_global_device_ids=true, to_apply=%region_3.0 | all-reduce | flops 327680 | bytes 1966080 | tf_op jit(solution)/shard_map/psum | solution.py:75
  50.4 0.8 fusion.45
  51.2 0.8 slice_convert_fusion
  52.1 0.0 copy-done.9
  52.1 0.1 reshape.146
  52.2 0.2 multiply_cosine_fusion
  52.4 0.1 subtract_convert_fusion
  52.5 0.7 pad_maximum_fusion
  53.2 5.3 %all-to-all-start = ((bf16[64,2,256]{2,1,0:T(2,128)(2,1)}), bf16[64,2,256]{2,1,0:T(2,128)(2,1)S(1)}, u32[]{:S(2)}, u32[]{:S(2)}) async-start(bf16[64,2,256]{2,1,0:T(2,128)(2,1)} %pad_maximum_fusion), calls=%async_computation | async-start | bytes 131072 | tf_op jit(solution)/shard_map/all_to_all | solution.py:84
  58.4 0.0 all-reduce.5.cloned.1.call-start
  58.4 0.1 dynamic_slice.14
  58.5 0.6 fusion.44
  59.1 0.1 iota_compare_fusion
  59.2 0.0 copy-start.6
  59.2 4.7 %all-to-all-done = bf16[64,2,256]{2,1,0:T(2,128)(2,1)S(1)} async-done(((bf16[64,2,256]{2,1,0:T(2,128)(2,1)}), bf16[64,2,256]{2,1,0:T(2,128)(2,1)S(1)}, u32[]{:S(2)}, u32[]{:S(2)}) %all-to-all-start) | async-done | bytes 65568 | tf_op jit(solution)/shard_map/all_to_all | solution.py:84
  64.1 0.1 fusion.24
  64.2 10.3 %select_reduce_fusion = (f32[4,8]{1,0:T(4,128)S(1)}, f32[4,8,8192]{2,1,0:T(8,128)S(1)}) fusion(pred[4,8192]{1,0:T(4,128)(4,1)S(1)} %iota_compare_fusion, bf16[4,8192,256]{2,1,0:T(8,128)(2,1)} %param.16, bf16[16,8,256]{2,1,0:T(8,128)(2,1)S(1)} %all_to_all.27, s32[]{:T(128)S(6)} %select_n.16), kind=kOutput, calls=%fused_computation.11 | convolution fusion | flops 135004128 | bytes 17875076 | tf_op jit(solution)/shard_map/bhe,bse->bhs/dot_general | solution.py:35
  74.5 0.0 copy-done.6
  74.5 0.4 fusion.1
  74.9 0.0 copy-start.3
  74.9 0.0 copy-start.8
  74.9 8.2 %fusion = bf16[4,8,256]{2,1,0:T(8,128)(2,1)S(1)} fusion(bf16[4,8192,256]{2,1,0:T(8,128)(2,1)} %param.17, f32[4,8,8192]{2,1,0:T(8,128)S(1)} %get-tuple-element.23, f32[4,8]{1,0:T(4,128)S(1)} %get-tuple-element.17, f32[4,8]{1,0:T(4,128)S(1)} %multiply_maximum_fusion, pred[4,8192]{1,0:T(4,128)(4,1)S(1)} %iota_compare_fusion, ...), kind=kOutput, calls=%fused_computation.8 | convolution fusion | flops 135290880 | bytes 17879424 | tf_op jit(solution)/shard_map/bhs,bse->bhe/dot_general | solution.py:44
  83.2 5.2 %all_gather.3 = bf16[16,8,256]{2,1,0:T(8,128)(2,1)S(1)} all-gather(bf16[4,8,256]{2,1,0:T(8,128)(2,1)S(1)} %fusion), channel_id=1, replica_groups=mesh['dp'=2,'yax'=4,'xax'=4] {'xax'}, dimensions={0}, use_global_device_ids=true | all-gather | bytes 81920 | tf_op jit(solution)/shard_map/all_gather | solution.py:90
  88.4 8.1 %all_to_all.33 = bf16[16,8,256]{2,0,1:T(8,128)(2,1)S(1)} all-to-all(bf16[16,8,256]{2,0,1:T(8,128)(2,1)S(1)} %copy.22), channel_id=1, replica_groups=mesh['dp'=2,'yax'=4,'xax'=4] {'yax'}, dimensions={1} | all-to-all | bytes 131072 | tf_op jit(solution)/shard_map/all_to_all | solution.py:91
  96.5 0.1 copy.23
  96.6 0.0 copy-done.3
  96.6 0.2 fusion.46
  96.8 0.0 copy-done.8
  96.8 0.0 copy-start.5
  96.8 2.1 convolution_add_fusion
  99.0 0.0 all-reduce.5.cloned.1.call-update
  99.0 0.0 all-reduce.7.cloned.1.call-start
  99.1 32.9 %all-reduce.5.cloned.1.call-done = f32[64,512]{1,0:T(8,128)} async-done(((f32[64,512]{1,0:T(8,128)}), f32[64,512]{1,0:T(8,128)}) %all-reduce.5.cloned.1.call-update) | async-done | bytes 131088 | tf_op jit(solution)/shard_map/psum | solution.py:96
  132.0 1.0 fusion.23
  133.0 5.7 %psum.38 = f32[2,64]{1,0:T(2,128)S(1)} all-reduce(f32[2,64]{1,0:T(2,128)S(1)} %pad_maximum_fusion.2), channel_id=1, replica_groups=mesh['dp'=2,'yax'=4,'xax'=4] {'xax'}, use_global_device_ids=true, to_apply=%region_9.10 | all-reduce | flops 128 | bytes 1024 | tf_op jit(solution)/shard_map/psum | solution.py:27
  138.7 0.0 copy-done.5
  138.7 10.4 %fusion.19 = f32[64,12576]{1,0:T(8,128)} fusion(bf16[12576,512]{1,0:T(8,128)(2,1)} %param.27, f32[512]{0:T(512)S(1)} %copy-done.5, f32[64]{0:T(128)S(1)} %fusion.33, f32[64]{0:T(128)S(1)} %multiply_bitcast_fusion, f32[64,512]{1,0:T(8,128)} %all-reduce.5.cloned.1.call-done, bf16[64,512]{1,0:T(8,128)(2,1)S(1)} %copy-done.1), kind=kOutput, calls=%fused_computation.41 | convolution fusion | flops 824377344 | bytes 16296448 | tf_op jit(solution)/shard_map/bd,vd->bv/dot_general | solution.py:98
  149.2 0.0 copy-start.10
  149.2 0.0 all-reduce.7.cloned.1.call-update
  149.2 0.6 copy-done.10
  149.8 0.6 dynamic-slice
  151.0 68.2 %all-reduce.7.cloned.1.call-done = f32[64,12576]{1,0:T(8,128)} async-done(((f32[64,12576]{1,0:T(8,128)}), f32[64,12576]{1,0:T(8,128)}) %all-reduce.7.cloned.1.call-update) | async-done | bytes 3219472
  219.2 1.5 dynamic-slice_reduce_fusion
  220.7 32.2 %pmax.7 = f32[64]{0:T(128)S(1)} all-reduce(f32[64]{0:T(128)S(1)} %dynamic-slice_reduce_fusion), channel_id=1, replica_groups=mesh['dp'=2,'yax'=4,'xax'=4] {'yax','xax'}, use_global_device_ids=true, to_apply=%region_12.13 | all-reduce | flops 64 | bytes 512 | tf_op jit(solution)/shard_map/pmax | solution.py:100
  253.0 1.6 exponential_reduce_fusion
  254.5 29.5 %psum.39 = f32[64]{0:T(128)S(1)} all-reduce(f32[64]{0:T(128)S(1)} %exponential_reduce_fusion), channel_id=1, replica_groups=mesh['dp'=2,'yax'=4,'xax'=4] {'yax','xax'}, use_global_device_ids=true, to_apply=%region_14.15 | all-reduce | flops 64 | bytes 512 | tf_op jit(solution)/shard_map/psum | solution.py:101
  284.0 2.3 dynamic-slice_subtract_fusion
  286.4 0.0 copy-done.7
  (17 shorter events, 0.2 us)
Async XLA Ops:
  7.2 13.6 %copy-start = (bf16[512,2048]{1,0:T(8,128)(2,1)S(1)}, bf16[512,2048]{1,0:T(8,128)(2,1)}, u32[]{:S(2)}) copy-start(bf16[512,2048]{1,0:T(8,128)(2,1)} %param.22) | copy-start | bytes 6291460
  16.8 5.3 %copy-start.1 = (bf16[64,512]{1,0:T(8,128)(2,1)S(1)}, bf16[64,512]{1,0:T(8,128)(2,1)}, u32[]{:S(2)}) copy-start(bf16[64,512]{1,0:T(8,128)(2,1)} %param.14) | copy-start | bytes 196612
  16.8 5.3 %copy-start.2 = (bf16[512,2048]{1,0:T(8,128)(2,1)S(1)}, bf16[512,2048]{1,0:T(8,128)(2,1)}, u32[]{:S(2)}) copy-start(bf16[512,2048]{1,0:T(8,128)(2,1)} %param.23) | copy-start | bytes 6291460
  16.8 5.3 %copy-start.4 = (f32[512]{0:T(512)S(1)}, f32[512]{0:T(512)}, u32[]{:S(2)}) copy-start(f32[512]{0:T(512)} %param.18) | copy-start | bytes 6148
  22.1 29.9 %copy-start.9 = (s32[64]{0:T(128)S(1)}, s32[64]{0:T(128)}, u32[]{:S(2)}) copy-start(s32[64]{0:T(128)} %param.15) | copy-start | bytes 772
  53.2 10.8 %all-to-all-start = ((bf16[64,2,256]{2,1,0:T(2,128)(2,1)}), bf16[64,2,256]{2,1,0:T(2,128)(2,1)S(1)}, u32[]{:S(2)}, u32[]{:S(2)}) async-start(bf16[64,2,256]{2,1,0:T(2,128)(2,1)} %pad_maximum_fusion), calls=%async_computation | async-start | bytes 131072 | tf_op jit(solution)/shard_map/all_to_all | solution.py:84
  58.4 73.6 %all-reduce.5.cloned.1.call-start = ((), (), s32[]{:S(2)}) async-start(), calls=%async_computation.2 | async-start | bytes 262144 | tf_op jit(solution)/shard_map/psum | solution.py:96
  59.2 15.2 %copy-start.6 = (bf16[4,256]{1,0:T(4,128)(2,1)}, bf16[4,256]{1,0:T(4,128)(2,1)S(1)}, u32[]{:S(2)}) copy-start(bf16[4,256]{1,0:T(4,128)(2,1)S(1)} %fusion.28) | copy-start | bytes 6148
  74.9 21.7 %copy-start.3 = (bf16[512,512]{1,0:T(8,128)(2,1)S(1)}, bf16[512,512]{1,0:T(8,128)(2,1)}, u32[]{:S(2)}) copy-start(bf16[512,512]{1,0:T(8,128)(2,1)} %param.24) | copy-start | bytes 1572868
  74.9 21.9 %copy-start.8 = (bf16[2048,512]{1,0:T(8,128)(2,1)S(1)}, bf16[2048,512]{1,0:T(8,128)(2,1)}, u32[]{:S(2)}) copy-start(bf16[2048,512]{1,0:T(8,128)(2,1)} %param.25) | copy-start | bytes 6291460
  96.8 41.9 %copy-start.5 = (f32[512]{0:T(512)S(1)}, f32[512]{0:T(512)}, u32[]{:S(2)}) copy-start(f32[512]{0:T(512)} %param.26) | copy-start | bytes 6148
  99.0 120.2 %all-reduce.7.cloned.1.call-start = ((), (), s32[]{:S(2)}) async-start(), calls=%async_computation.3 | async-start | bytes 6488064
  149.2 0.7 copy-start.10
  284.0 2.3 copy-start.7
Sparse Core Ops, SparseCore 0:
  99.1 32.7 all-reduce.4
  149.3 69.8 all-reduce.6
where the time goes:
time: 294 us; the launch traced here: 293 us
  blocking collectives  117 us (40%)
  waiting for transfers between devices  106 us (36%)
  matrix products  37.2 us (13%)
  between operations  15 us (5%)
  other arithmetic  11.4 us (4%)
  starting transfers between devices  5.3 us (2%)
    unnamed x3, waiting for transfers between devices  68.2 us
    psum x1, waiting for transfers between devices, local_step(): residual_out = residual + lax.psum(branch_sum, 'yax')  32.9 us
    pmax x1, blocking collectives, local_step(): row_max = lax.pmax(jnp.max(logits, axis=1), ('yax', 'xax'))  32.2 us
    psum x1, blocking collectives, local_step(): lax.psum(jnp.sum(jnp.exp(logits - row_max[:, None]), axis=1), ('yax', 'xa...  29.5 us
    psum x1, blocking collectives, local_step(): projected = lax.psum(proj_part, 'xax').astype(jnp.bfloat16)  27.8 us
    psum x2, blocking collectives, sharded_norm(): stats = lax.psum(stats, 'xax')  14.1 us
    dot_general x1, matrix products, local_step(): jnp.einsum('bd,vd->bv', final_norm, embedding, preferred_element_type=jnp...  10.4 us
    dot_general x1, matrix products, attend_local(): jnp.einsum('bhe,bse->bhs', query, k_cache, preferred_element_type=jnp.flo...  10.3 us
  transfers between devices with their start and end apart: 3, of which 3 were waited for; matrix products, arithmetic and copies ran while one was open for 0% of the time, Pallas kernels for 0%

commit v1 on v0

v1 whole, which is shorter than its diff:
```python
import functools

import jax
import jax.numpy as jnp
from jax import lax
from jax.experimental import pallas as pl
from jax.experimental.pallas import tpu as pltpu
from jax.sharding import PartitionSpec as P

EPS = 1e-6
ROPE_BASE = 10000.0
F32 = jnp.float32
BF16 = jnp.bfloat16
MESH = pl.DeviceIdType.MESH


def rope_angle(positions, head_dim):
    half_dim = head_dim // 2
    inv_freq = ROPE_BASE ** (-(jnp.arange(half_dim, dtype=jnp.float32) * 2.0) / head_dim)
    return positions.astype(jnp.float32)[:, None] * inv_freq[None, :]


def dot(a, b):
    return jnp.dot(a, b, preferred_element_type=F32)


def dot_t(a, b):
    return lax.dot_general(a, b, (((1,), (1,)), ((), ())), preferred_element_type=F32)


def one_hot_rows(rows, cols, source):
    r = lax.broadcasted_iota(jnp.int32, (rows, cols), 0)
    c = lax.broadcasted_iota(jnp.int32, (rows, cols), 1)
    return jnp.where(c == source(r), 1.0, 0.0).astype(BF16)


def step_kernel(sizes,
                lens, hidden_hbm, table_hbm, k_hbm, v_hbm, ga_hbm, wq_hbm, wk_hbm, wv_hbm, wg_hbm, wu_hbm,
                wo_hbm, wd_hbm, gf_hbm, emb_hbm,
                kn_out, vn_out, z_out, ln_out,
                hid, table, ga, gf, kbuf, vbuf, wq, wkv, wg, wu, wo, wd,
                st_send, st_recv, qkv, qkv_recv, q_send, q_recv, qs, kns, vns, os_, o_send, o_recv,
                gup, gu_recv, gux, gux_recv, m_all, mdown, bpart, b_recv, s2_send, s2_recv, fbuf,
                lsend1, lrecv1, hold, xrecv, lsend2, lrecv2, own, l_send, l_recv,
                ld_sem, kv_sem, e_sem, send_sem, st_sem, qkv_sem, q_sem, gu_sem, gux_sem, m_sem, o_sem,
                b_sem, s2_sem, f_sem, l1_sem, lx_sem, l2_sem, lse_sem):
    rows, wid, seq, hd, ffc, vb, chunks = sizes
    yi = lax.axis_index("yax")
    xi = lax.axis_index("xax")
    x1 = xi + 1 - 2 * (xi % 2)
    x2 = (xi + 2) % 4
    x3 = (x1 + 2) % 4
    me = yi * 4 + xi
    ypeers = [(yi + d) % 4 for d in (1, 2, 3)]
    xpeers = [x1, x2, x3]

    loads = {}

    def load(name, i, src, dst):
        loads[name] = pltpu.make_async_copy(src, dst, ld_sem.at[i])
        loads[name].start()

    load("hid", 0, hidden_hbm, hid)
    load("ga", 1, ga_hbm, ga)
    load("table", 2, table_hbm, table)
    load("wq", 3, wq_hbm, wq)
    load("wk", 4, wk_hbm, wkv.at[0])
    load("wv", 5, wv_hbm, wkv.at[1])
    n_id = 6
    for i, xx in enumerate((x1, x3, x2, xi)):
        cols = pl.ds(pl.multiple_of(xx * ffc, ffc), ffc)
        load(f"wg{i}", n_id, wg_hbm.at[:, cols], wg.at[xx])
        load(f"wu{i}", n_id + 1, wu_hbm.at[:, cols], wu.at[xx])
        n_id += 2
    barrier = pltpu.get_barrier_semaphore()
    for dy in range(4):
        for dx in range(4):
            if dy or dx:
                pl.semaphore_signal(barrier, inc=1,
                                    device_id={"yax": (yi + dy) % 4, "xax": (xi + dx) % 4}, device_id_type=MESH)
    for j in range(4):
        pltpu.make_async_copy(k_hbm.at[j], kbuf.at[j], kv_sem.at[j]).start()
        pltpu.make_async_copy(v_hbm.at[j], vbuf.at[j], kv_sem.at[4 + j]).start()
    load("wd", n_id, wd_hbm, wd)
    load("wo", n_id + 1, wo_hbm, wo)
    load("gf", n_id + 2, gf_hbm, gf)

    sends = []

    def send(src, dst, rsem, yy, xx):
        cp = pltpu.make_async_remote_copy(src_ref=src, dst_ref=dst, send_sem=send_sem.at[len(sends)], recv_sem=rsem,
                                          device_id={"yax": yy, "xax": xx}, device_id_type=MESH)
        cp.start()
        sends.append(cp)

    def recv(dst, rsem):
        pltpu.make_async_copy(dst, dst, rsem).wait()

    loads["hid"].wait()
    loads["ga"].wait()
    h = hid[...].astype(F32)
    mean_l = jnp.sum(h, axis=1, keepdims=True) * (1.0 / wid)
    dev = h - mean_l
    m2_l = jnp.sum(dev * dev, axis=1, keepdims=True)
    lane = lax.broadcasted_iota(jnp.int32, (rows, 128), 1)
    stat = jnp.where(lane == 0, mean_l, m2_l)
    stat_t = jnp.concatenate([stat, stat], axis=0).T[:8]
    st_send[...] = stat_t
    pl.semaphore_wait(barrier, 15)
    for xx in xpeers:
        send(st_send, st_recv.at[xi], st_sem.at[xi], yi, xx)
    perm = one_hot_rows(96, 64, lambda r: jnp.where(
        r % 24 < 16, ((r % 24) // 4) * 16 + (r // 24) * 4 + r % 4,
        jnp.where(r % 24 < 20, yi * 16 + (r // 24) * 4 + r % 4, -1)))
    for xx in xpeers:
        recv(st_recv.at[xx], st_sem.at[xx])
    parts = [stat_t] + [st_recv[xx] for xx in xpeers]
    means = [p[0:1] for p in parts]
    mu = (means[0] + means[1] + means[2] + means[3]) * 0.25
    m2 = sum([p[1:2] for p in parts]) + wid * sum([(m - mu) * (m - mu) for m in means])
    rstd = lax.rsqrt(m2 * (1.0 / (4 * wid)) + EPS)
    sub = lax.broadcasted_iota(jnp.int32, (128, 128), 0)
    cols_t = jnp.where(sub == 0, mu, rstd).T
    mu_c = cols_t[:rows, 0:1]
    rstd_c = cols_t[:rows, 1:2]
    normed = ((h - mu_c) * rstd_c * ga[...]).astype(BF16)
    n_perm = dot(perm, normed).astype(BF16)

    loads["wq"].wait()
    loads["wk"].wait()
    loads["wv"].wait()
    q_part = dot(n_perm, wq[...])
    kv_part = jnp.concatenate([dot(n_perm, wkv[0]), dot(n_perm, wkv[1])], axis=1)
    prow = lax.broadcasted_iota(jnp.int32, (96, 2 * hd), 0)
    qkv[...] = jnp.where(prow % 24 < 16, q_part, kv_part).reshape(4, 24, 2 * hd)
    for xx in (x2, x3, x1):
        send(qkv.at[xx], qkv_recv.at[xi], qkv_sem.at[xi], yi, xx)

    for i, xx in enumerate((x1, x3, x2, xi)):
        loads[f"wg{i}"].wait()
        loads[f"wu{i}"].wait()
        gup[xx, 0] = dot(normed, wg[xx])
        gup[xx, 1] = dot(normed, wu[xx])
        if i < 2:
            send(gup.at[xx], gu_recv.at[i], gu_sem.at[i], yi, x1)

    loads["table"].wait()
    for xx in (x1, x2, x3):
        recv(qkv_recv.at[xx], qkv_sem.at[xx])
    tot = ((qkv[xi] + qkv_recv[x1]) + (qkv_recv[x2] + qkv_recv[x3])).astype(BF16).astype(F32)
    half = hd // 2
    cos_a = table[:, :half]
    sin_a = table[:, half:]
    lo0, hi0, lo1, hi1 = [tot[:, i * half:(i + 1) * half] for i in range(4)]
    r0 = (lo0 * cos_a - hi0 * sin_a).astype(BF16)
    r1 = (hi0 * cos_a + lo0 * sin_a).astype(BF16)
    r2 = (lo1 * cos_a - hi1 * sin_a).astype(BF16)
    r3 = (hi1 * cos_a + lo1 * sin_a).astype(BF16)
    kns[:, :half] = r0[16:].astype(F32)
    kns[:, half:] = r1[16:].astype(F32)
    vns[...] = tot[16:, hd:]
    stacked = jnp.concatenate([r0[:16], r1[:16], r2[:16], r3[:16]], axis=0)
    s1 = one_hot_rows(64, 64, lambda r: ((r // 4) % 4) * 16 + (r // 16) * 4 + r % 4)
    q_send[...] = dot(s1, stacked).astype(BF16).reshape(4, 16, 128)
    for yy in ypeers:
        send(q_send.at[yy], q_recv.at[yi], q_sem.at[yi], yy, xi)
    q_recv[yi] = q_send[yi]
    kn_out[...] = kns[...].astype(BF16)[:4]
    vn_out[...] = vns[...].astype(BF16)[:4]

    recv(gu_recv.at[1], gu_sem.at[1])
    gux[...] = gup[x2] + gu_recv[1]
    send(gux, gux_recv, gux_sem, yi, x2)
    recv(gu_recv.at[0], gu_sem.at[0])

    for yy in ypeers:
        recv(q_recv.at[yy], q_sem.at[yy])
    s2 = one_hot_rows(64, 64, lambda r: ((r // 2) % 4) * 16 + (r % 2) * 8 + (r // 32) * 4 + (r // 8) % 4)
    q_all = dot(s2, q_recv[...].reshape(64, 128))
    qs[...] = jnp.concatenate([q_all[:32], q_all[32:]], axis=1).reshape(4, 8, hd)

    scale = hd ** -0.5
    pos = lax.broadcasted_iota(jnp.int32, (8, seq), 1)

    def attend(j, carry):
        qj = qs[j]
        length = lens[me * 4 + j]
        pltpu.make_async_copy(k_hbm.at[j], kbuf.at[j], kv_sem.at[j]).wait()
        s = dot_t(qj.astype(BF16), kbuf[j]) * scale
        s_new = jnp.sum(qj * kns[pl.ds(j, 1), :], axis=1, keepdims=True) * scale
        s = jnp.where(pos < length, s, -jnp.inf)
        top = jnp.maximum(jnp.max(s, axis=1, keepdims=True), s_new)
        w = jnp.exp(s - top)
        w_new = jnp.exp(s_new - top)
        inv = 1.0 / (jnp.sum(w, axis=1, keepdims=True) + w_new)
        prob = (w * inv).astype(BF16)
        p_new = (w_new * inv).astype(BF16).astype(F32)
        pltpu.make_async_copy(v_hbm.at[j], vbuf.at[j], kv_sem.at[4 + j]).wait()
        os_[j] = dot(prob, vbuf[j]) + p_new * vns[pl.ds(j, 1), :]
        voc = pl.ds(pl.multiple_of(j * vb, 8), vb)
        pltpu.make_async_copy(emb_hbm.at[voc, pl.ds(0, hd)], kbuf.at[j, pl.ds(0, vb)], e_sem.at[j]).start()
        pltpu.make_async_copy(emb_hbm.at[voc, pl.ds(hd, hd)], vbuf.at[j, pl.ds(0, vb)], e_sem.at[4 + j]).start()
        return carry

    lax.fori_loop(0, 2, attend, 0)
    recv(gux_recv, gux_sem)
    gu = gup[xi] + gu_recv[0] + gux_recv[...]
    gate = gu[0].astype(BF16).astype(F32)
    up_val = gu[1].astype(BF16).astype(F32)
    m_all[xi] = (gate * jax.nn.sigmoid(gate) * up_val).astype(BF16)
    for xx in (x2, x3, x1):
        send(m_all.at[xi], m_all.at[xi], m_sem.at[xi], yi, xx)
    lax.fori_loop(2, 4, attend, 0)

    o_bf = os_[...].reshape(32, hd).astype(BF16)
    s3 = one_hot_rows(64, 64, lambda r: ((r // 4) % 2) * 32 + (r % 4) * 8 + (r // 16) * 2 + (r // 8) % 2)
    o_send[...] = dot(s3, jnp.concatenate([o_bf[:, :half], o_bf[:, half:]], axis=0)).astype(BF16).reshape(4, 16, 128)
    for yy in ypeers:
        for xx in (x3, x2, x1, xi):
            send(o_send.at[yy], o_recv.at[me], o_sem.at[me], yy, xx)
    for xx in xpeers:
        send(o_send.at[yi], o_recv.at[me], o_sem.at[me], yi, xx)
    o_recv[me] = o_send[yi]

    loads["wd"].wait()
    loads["wo"].wait()
    loads["gf"].wait()
    for xx in xpeers:
        recv(m_all.at[xx], m_sem.at[xx])
    mdown[...] = sum([dot(m_all[i], wd[pl.ds(i * ffc, ffc)]) for i in range(4)])
    s4 = one_hot_rows(256, 256, lambda r: ((r % 64) // 4) * 16 + (r // 64) * 4 + r % 4)
    for xx in xpeers:
        recv(o_recv.at[yi * 4 + xx], o_sem.at[yi * 4 + xx])
    for yy in ypeers:
        for xx in (xi, x1, x2, x3):
            recv(o_recv.at[yy * 4 + xx], o_sem.at[yy * 4 + xx])
    a_all = dot(s4, o_recv[...].reshape(256, 128)).astype(BF16)
    attn = jnp.concatenate([a_all[i * 64:(i + 1) * 64] for i in range(4)], axis=1)
    bpart[...] = (dot(attn, wo[...]) + mdown[...]).reshape(4, 16, wid)
    for yy in (ypeers[1], ypeers[0], ypeers[2]):
        send(bpart.at[yy], b_recv.at[yi], b_sem.at[yi], yy, xi)
    res = hid[pl.ds(pl.multiple_of(yi * 16, 16), 16), :].astype(F32)
    for yy in ypeers:
        recv(b_recv.at[yy], b_sem.at[yy])
    res = res + ((bpart[yi] + b_recv[ypeers[0]]) + (b_recv[ypeers[1]] + b_recv[ypeers[2]]))

    mean_l = jnp.sum(res, axis=1, keepdims=True) * (1.0 / wid)
    dev = res - mean_l
    m2_l = jnp.sum(dev * dev, axis=1, keepdims=True)
    lane = lax.broadcasted_iota(jnp.int32, (16, 128), 1)
    s2_send[...] = jnp.where(lane < 64, mean_l, m2_l)
    for xx in xpeers:
        send(s2_send, s2_recv.at[xi], s2_sem.at[xi], yi, xx)
    for xx in xpeers:
        recv(s2_recv.at[xx], s2_sem.at[xx])
    parts = [s2_recv[xx] for xx in xpeers]
    means = [mean_l] + [p[:, 0:1] for p in parts]
    mu = (means[0] + means[1] + means[2] + means[3]) * 0.25
    m2 = m2_l + sum([p[:, 64:65] for p in parts]) + wid * sum([(m - mu) * (m - mu) for m in means])
    rstd = lax.rsqrt(m2 * (1.0 / (4 * wid)) + EPS)
    fbuf[yi] = ((res - mu) * rstd * gf[...]).astype(BF16)
    for yy in ypeers:
        send(fbuf.at[yi], fbuf.at[yi], f_sem.at[yi], yy, xi)
    for j in range(4):
        pltpu.make_async_copy(emb_hbm.at[pl.ds(0, vb), pl.ds(0, hd)], kbuf.at[j, pl.ds(0, vb)], e_sem.at[j]).wait()
        pltpu.make_async_copy(emb_hbm.at[pl.ds(0, vb), pl.ds(0, hd)], vbuf.at[j, pl.ds(0, vb)], e_sem.at[4 + j]).wait()
    for yy in ypeers:
        recv(fbuf.at[yy], f_sem.at[yy])
    f = fbuf[...].reshape(rows, wid)
    f0 = f[:, :hd]
    f1 = f[:, hd:]

    def logit_part(xx, c0, cn):
        voc = pl.ds(c0, cn)
        return dot_t(f0, kbuf[xx, voc]) + dot_t(f1, vbuf[xx, voc])

    def cross(i):
        c0, cn = chunks[i]
        cs = pl.ds(c0, cn)
        recv(lrecv1.at[:, cs], l1_sem.at[i])
        hold[:, cs] = hold[:, cs] + lrecv1[:, cs]
        send(hold.at[:, cs], xrecv.at[:, cs], lx_sem.at[i], yi, x2)

    for i, (c0, cn) in enumerate(chunks):
        cs = pl.ds(c0, cn)
        lsend1[:, cs] = logit_part(x3, c0, cn)
        send(lsend1.at[:, cs], lrecv1.at[:, cs], l1_sem.at[i], yi, x1)
        hold[:, cs] = logit_part(x2, c0, cn)
        if i >= 1:
            cross(i - 1)
    cross(len(chunks) - 1)
    for i, (c0, cn) in enumerate(chunks):
        cs = pl.ds(c0, cn)
        lsend2[:, cs] = logit_part(x1, c0, cn)
        send(lsend2.at[:, cs], lrecv2.at[:, cs], l2_sem.at[i], yi, x1)
        own[:, cs] = logit_part(xi, c0, cn)
    m_run = jnp.full((rows, 1), -jnp.inf, F32)
    s_run = jnp.zeros((rows, 1), F32)
    for i, (c0, cn) in enumerate(chunks):
        cs = pl.ds(c0, cn)
        recv(lrecv2.at[:, cs], l2_sem.at[i])
        recv(xrecv.at[:, cs], lx_sem.at[i])
        z = own[:, cs] + lrecv2[:, cs] + xrecv[:, cs]
        if c0 + cn > vb:
            z_out[:, c0:vb] = z[:, :vb - c0]
            z = jnp.where(lax.broadcasted_iota(jnp.int32, (rows, cn), 1) < vb - c0, z, -jnp.inf)
        else:
            z_out[:, cs] = z
        m_new = jnp.maximum(m_run, jnp.max(z, axis=1, keepdims=True))
        s_run = s_run * jnp.exp(m_run - m_new) + jnp.sum(jnp.exp(z - m_new), axis=1, keepdims=True)
        m_run = m_new

    lane = lax.broadcasted_iota(jnp.int32, (rows, 128), 1)
    stat = jnp.where(lane == 0, m_run, s_run)
    mine = jnp.concatenate([stat, stat], axis=0).T[0:2]
    l_send[...] = mine
    for yy in ypeers:
        for xx in (x3, x2, x1, xi):
            send(l_send, l_recv.at[me], lse_sem.at[me], yy, xx)
    for xx in xpeers:
        send(l_send, l_recv.at[me], lse_sem.at[me], yi, xx)
    l_recv[me] = mine
    for xx in xpeers:
        recv(l_recv.at[yi * 4 + xx], lse_sem.at[yi * 4 + xx])
    for yy in ypeers:
        for xx in (xi, x1, x2, x3):
            recv(l_recv.at[yy * 4 + xx], lse_sem.at[yy * 4 + xx])
    tops = [l_recv[i, 0:1, :] for i in range(16)]
    top = functools.reduce(jnp.maximum, tops)
    total = sum([l_recv[i, 1:2, :] * jnp.exp(tops[i] - top) for i in range(16)])
    log_norm = top + jnp.log(total)
    ln_out[...] = jnp.broadcast_to(log_norm, (128, 128)).T[:rows, 0:1]
    for cp in sends:
        cp.wait_send()


def solution(mesh):
    row_spec = P(("dp", "yax", "xax"))

    def local_step(hidden, cache_len, k_cache, v_cache, g_attn, w_query, w_key, w_value,
                   w_gate, w_up, w_out, w_down, g_final, embedding):
        rows, wid = hidden.shape
        own_rows, seq, hd = k_cache.shape
        ffc = w_gate.shape[1] // 4
        vb = embedding.shape[0] // 4
        y_idx = lax.axis_index("yax")
        x_idx = lax.axis_index("xax")
        lens3 = cache_len.reshape(4, 4, 4)
        lens_x = lax.dynamic_index_in_dim(lens3, x_idx, axis=1, keepdims=False)
        lens_me = lax.dynamic_index_in_dim(lens_x, y_idx, axis=0, keepdims=False)
        angles = rope_angle(jnp.concatenate([lens_x.reshape(16), lens_me, lens_me]), hd)
        table = jnp.concatenate([jnp.cos(angles), jnp.sin(angles)], axis=1)
        vbp = -(-vb // 128) * 128
        chunks = [(c, min(512, vbp - c)) for c in range(0, vbp, 512)]
        nch = len(chunks)
        sizes = (rows, wid, seq, hd, ffc, vb, chunks)
        any_spec = pl.BlockSpec(memory_space=pl.ANY)
        vmem = pl.BlockSpec(memory_space=pltpu.VMEM)
        v = pltpu.VMEM
        dma = pltpu.SemaphoreType.DMA
        scratch = [
            v((rows, wid), BF16), v((24, hd), F32), v((1, wid), F32), v((1, wid), F32),
            v((4, seq, hd), BF16), v((4, seq, hd), BF16),
            v((wid, 2 * hd), BF16), v((2, wid, hd), BF16), v((4, wid, ffc), BF16), v((4, wid, ffc), BF16),
            v((2 * hd, wid), BF16), v((4 * ffc, wid), BF16),
            v((8, 128), F32), v((4, 8, 128), F32), v((4, 24, 2 * hd), F32), v((4, 24, 2 * hd), F32),
            v((4, 16, 128), BF16), v((4, 16, 128), BF16), v((4, 8, hd), F32), v((8, hd), F32), v((8, hd), F32),
            v((4, 8, hd), F32), v((4, 16, 128), BF16), v((16, 16, 128), BF16),
            v((4, 2, rows, ffc), F32), v((2, 2, rows, ffc), F32), v((2, rows, ffc), F32), v((2, rows, ffc), F32),
            v((4, rows, ffc), BF16), v((rows, wid), F32), v((4, 16, wid), F32), v((4, 16, wid), F32),
            v((16, 128), F32), v((4, 16, 128), F32), v((4, 16, wid), BF16),
            v((rows, vbp), F32), v((rows, vbp), F32), v((rows, vbp), F32), v((rows, vbp), F32),
            v((rows, vbp), F32), v((rows, vbp), F32), v((rows, vbp), F32),
            v((2, 128), F32), v((16, 2, 128), F32),
            dma((20,)), dma((8,)), dma((8,)), dma((100,)), dma((4,)), dma((4,)), dma((4,)), dma((2,)), dma(()),
            dma((4,)), dma((16,)), dma((4,)), dma((4,)), dma((4,)), dma((nch,)), dma((nch,)), dma((nch,)), dma((16,)),
        ]
        k_new, v_new, z, ln = pl.pallas_call(
            functools.partial(step_kernel, sizes),
            name="decode_step",
            out_shape=(jax.ShapeDtypeStruct((own_rows, hd), BF16), jax.ShapeDtypeStruct((own_rows, hd), BF16),
                       jax.ShapeDtypeStruct((rows, vb), F32), jax.ShapeDtypeStruct((rows, 1), F32)),
            in_specs=[pl.BlockSpec(memory_space=pltpu.SMEM)] + [any_spec] * 14,
            out_specs=(vmem, vmem, vmem, vmem),
            scratch_shapes=scratch,
            compiler_params=pltpu.CompilerParams(collective_id=0, has_side_effects=True,
                                                 vmem_limit_bytes=60 * 1024 * 1024),
        )(cache_len, hidden, table, k_cache, v_cache, g_attn.reshape(1, wid), w_query, w_key, w_value,
          w_gate, w_up, w_out, w_down, g_final.reshape(1, wid), embedding)
        return k_new, v_new, z - ln, ln[:, 0]

    in_specs = (P("dp", "xax"), P("dp"), row_spec, row_spec, P("xax"), P("xax", "yax"),
                P("xax", None), P("xax", None), P("xax", "yax"), P("xax", "yax"),
                P("yax", "xax"), P("yax", "xax"), P("xax"), P("yax", "xax"))
    out_specs = (row_spec, row_spec, P("dp", ("yax", "xax")), P("dp"))
    return jax.shard_map(local_step, mesh=mesh, in_specs=in_specs, out_specs=out_specs, check_vma=False)
```

time: 294 us -> 82.5 us (0.28)
  blocking collectives: 117 us -> 0 us
  waiting for transfers between devices: 106 us -> 0 us
  Pallas kernels: 0 us -> 74.3 us
  matrix products: 37.2 us -> 0 us
  between operations: 15 us -> 0.68 us
  other arithmetic: 11.4 us -> 3.86 us
  starting transfers between devices: 5.3 us -> 0 us
    pallas_call x0 -> x1, Pallas kernels: none -> 74.3 us  [local_step(): pl.pallas_call(functools.partial(step_kernel, sizes), name='decode_step',...]
    psum x4 -> x0, blocking collectives: 71.4 us -> none  [the longest x1 29.5 us: local_step(): lax.psum(jnp.sum(jnp.exp(logits - row_max[:, None]), axis=1), ('yax', 'xa...]
    unnamed x3 -> x0, waiting for transfers between devices: 68.2 us -> none
    dot_general x11 -> x0, matrix products: 37.2 us -> none  [the longest x1 10.4 us: local_step(): jnp.einsum('bd,vd->bv', final_norm, embedding, preferred_element_type=jnp...]
    psum x1 -> x0, waiting for transfers between devices: 32.9 us -> none  [local_step(): residual_out = residual + lax.psum(branch_sum, 'yax')]
    pmax x1 -> x0, blocking collectives: 32.2 us -> none  [local_step(): row_max = lax.pmax(jnp.max(logits, axis=1), ('yax', 'xax'))]
    all_to_all x1 -> x0, blocking collectives: 8.11 us -> none  [local_step(): lax.all_to_all(attn_grp, 'yax', 1, 0, tiled=True).reshape(rows, q_cols)]
    all_to_all x1 -> x0, starting transfers between devices: 5.26 us -> none  [local_step(): query_grp = lax.all_to_all(query, 'yax', 0, 1, tiled=True)]
  transfers between devices with their start and end apart: 3 -> 0, of which waited for: 3 -> 0; matrix products, arithmetic and copies ran while one was open for 0% -> 0% of each run, Pallas kernels for 0% -> 0%
where the time goes in v1:
time: 82.5 us; the launch traced here: 82.3 us
  Pallas kernels  74.3 us (90%)
  other arithmetic  3.86 us (5%)
  local copies, waits for them, and re-layouts  3.37 us (4%)
    pallas_call x1, Pallas kernels, local_step(): pl.pallas_call(functools.partial(step_kernel, sizes), name='decode_step',...  74.3 us
    unnamed x4, local copies, waits for them, and re-layouts  2.5 us
    sub x1, other arithmetic, local_step(): return (k_new, v_new, z - ln, ln[:, 0])  2.16 us

profile of v1, /device:TPU:0, one launch (start us, length us, event | category | flops | bytes accessed | tf_op | source)
XLA Modules:
  0.0 82.3 jit_solution(3522134883716769651)
XLA Ops:
  0.7 0.7 reshape.53
  1.4 0.1 concatenate.14
  1.5 0.1 add_convert_fusion
  1.6 0.1 multiply_cosine_fusion
  1.7 0.6 pad_maximum_fusion.table_hbm
  2.4 74.3 %decode_step.1 = (bf16[4,256]{1,0:T(4,128)(2,1)}, bf16[4,256]{1,0:T(4,128)(2,1)}, f32[64,3144]{1,0:T(8,128)}, f32[64,1]{1,0:T(8,128)}) custom-call(s32[64]{0:T(128)} %lens.1, bf16[64,512]{1,0:T(8,128)(2,1)} %hidden_hbm.1, f32[24,256]{1,0:T(8,128)} %pad_maximum_fusion.table_hbm, bf16[4,8192,256]{2,1,0:T(8,128)(2,1)} %k_hbm.1, bf16[4,8192,256]{2,1,0:T(8,128)(2,1)} %v_hbm.1, ...), custom_call_target="tpu_custom_call" | custom-call | tf_op jit(solution)/shard_map/decode_step/pallas_call | solution.py:378
  76.7 0.9 %reduce.1 = f32[64]{0:T(128)S(1)} reduce(f32[64,1]{1,0:T(8,128)} %get-tuple-element.11, f32[]{:T(128)} %constant.44), dimensions={1}, to_apply=%get-tuple-element.11.reduce_sub_computation | reduce | bytes 516 | tf_op jit(solution)/shard_map/decode_step/pallas_call | solution.py:378
  77.6 0.0 copy-start
  77.6 2.2 %broadcast_subtract_fusion = f32[64,3144]{1,0:T(8,128)} fusion(f32[64,3144]{1,0:T(8,128)} %get-tuple-element.10, f32[64]{0:T(128)S(1)} %reduce.1), kind=kLoop, calls=%fused_computation | loop fusion | flops 201216 | bytes 1609984 | tf_op jit(solution)/shard_map/sub | solution.py:390
  79.8 1.2 %copy.20 = bf16[4,256]{1,0:T(4,128)(2,1)} copy(bf16[4,256]{1,0:T(4,128)(2,1)} %get-tuple-element.18) | data formatting | bytes 4096
  81.0 1.2 %copy.21 = bf16[4,256]{1,0:T(4,128)(2,1)} copy(bf16[4,256]{1,0:T(4,128)(2,1)} %get-tuple-element.19) | data formatting | bytes 4096
  82.2 0.0 copy-done
  (3 shorter events, 0.0 us)
Async XLA Ops:
  77.6 4.7 %copy-start = (f32[64]{0:T(128)}, f32[64]{0:T(128)S(1)}, u32[]{:S(2)}) copy-start(f32[64]{0:T(128)S(1)} %reduce.1) | copy-start | bytes 772

commit v2 on v1

v2 whole, which is shorter than its diff:
```python
import functools

import jax
import jax.numpy as jnp
from jax import lax
from jax.experimental import pallas as pl
from jax.experimental.pallas import tpu as pltpu
from jax.sharding import PartitionSpec as P

EPS = 1e-6
ROPE_BASE = 10000.0
F32 = jnp.float32
BF16 = jnp.bfloat16
MESH = pl.DeviceIdType.MESH


def dot(a, b):
    return jnp.dot(a, b, preferred_element_type=F32)


def dot_t(a, b):
    return lax.dot_general(a, b, (((1,), (1,)), ((), ())), preferred_element_type=F32)


def one_hot_rows(rows, cols, source):
    r = lax.broadcasted_iota(jnp.int32, (rows, cols), 0)
    c = lax.broadcasted_iota(jnp.int32, (rows, cols), 1)
    return jnp.where(c == source(r), 1.0, 0.0).astype(BF16)


def step_kernel(sizes,
                lens, hidden_hbm, freq_hbm, k_hbm, v_hbm, ga_hbm, wq_hbm, wk_hbm, wv_hbm, wg_hbm, wu_hbm,
                wo_hbm, wd_hbm, gf_hbm, emb_hbm,
                kv_out, z_out, ln_out, lr_out,
                hid, freq, table, ga, gf, kbuf, vbuf, wq, wkv, wgu, wo, wd,
                st_send, st_recv, qkv, qkv_recv, q_send, q_recv, qs, kns, vns, os_, sbuf, o_send, o_recv,
                gup, gu_recv, gux, gux_recv, m_all, mdown, bpart, b_recv, s2_send, s2_recv, fbuf,
                lsend1, lrecv1, hold, xrecv, lsend2, lrecv2, own, lcol, l_send, l_recv,
                ld_sem, snd_sem, rcv_sem, l1_sem, lx_sem, l2_sem):
    rows, wid, seq, hd, ffc, vb, chunks_a, chunks_b, chunks_c = sizes
    yi = lax.axis_index("yax")
    xi = lax.axis_index("xax")
    x1 = xi + 1 - 2 * (xi % 2)
    x2 = (xi + 2) % 4
    x3 = (x1 + 2) % 4
    me = yi * 4 + xi
    ypeers = [(yi + d) % 4 for d in (1, 2, 3)]
    xpeers = [x1, x2, x3]

    def load(i, *pairs):
        for src, dst in pairs:
            pltpu.make_async_copy(src, dst, ld_sem.at[i]).start()

    def loaded(i, dst):
        pltpu.make_async_copy(dst, dst, ld_sem.at[i]).wait()

    HID, GA, FREQ, WQ, WKV, WGU, WD, WO, GF, KEY, VAL, EK, EV = 0, 1, 2, 3, 4, 5, 9, 10, 11, 12, 13, 14, 15
    load(HID, (hidden_hbm, hid))
    load(GA, (ga_hbm, ga))
    barrier = pltpu.get_barrier_semaphore()
    for dy in range(4):
        for dx in range(4):
            if dy or dx:
                pl.semaphore_signal(barrier, inc=1,
                                    device_id={"yax": (yi + dy) % 4, "xax": (xi + dx) % 4}, device_id_type=MESH)
    load(FREQ, (freq_hbm, freq))
    load(WQ, (wq_hbm, wq))
    load(WKV, (wk_hbm, wkv.at[0]), (wv_hbm, wkv.at[1]))
    for i, xx in enumerate((x1, x3, x2, xi)):
        cols = pl.ds(pl.multiple_of(xx * ffc, ffc), ffc)
        load(WGU + i, (wg_hbm.at[:, cols], wgu.at[xx, 0]), (wu_hbm.at[:, cols], wgu.at[xx, 1]))
    load(KEY, *[(k_hbm.at[j], kbuf.at[j]) for j in range(4)])
    load(VAL, *[(v_hbm.at[j], vbuf.at[j]) for j in range(4)])
    load(WD, (wd_hbm, wd))
    load(WO, (wo_hbm, wo))
    load(GF, (gf_hbm, gf))

    ST, QKV, Q, GU, GUX, M, O, B, S2, FN, LSE, L1, LX, L2 = range(14)

    def send(src, dst, i, yy, xx, rsem=None):
        pltpu.make_async_remote_copy(src_ref=src, dst_ref=dst, send_sem=snd_sem.at[i],
                                     recv_sem=rcv_sem.at[i] if rsem is None else rsem,
                                     device_id={"yax": yy, "xax": xx}, device_id_type=MESH).start()

    def recv(dst, i):
        pltpu.make_async_copy(dst, dst, rcv_sem.at[i]).wait()

    def recv_chunk(dst, sem):
        pltpu.make_async_copy(dst, dst, sem).wait()

    def sent(src, i):
        pltpu.make_async_copy(src, src, snd_sem.at[i]).wait()

    three = pl.ds(0, 3)
    most = pl.ds(0, 15)

    loaded(HID, hid)
    loaded(GA, ga)
    h = hid[...].astype(F32)
    mean_l = jnp.sum(h, axis=1, keepdims=True) * (1.0 / wid)
    dev = h - mean_l
    m2_l = jnp.sum(dev * dev, axis=1, keepdims=True)
    lane = lax.broadcasted_iota(jnp.int32, (rows, 128), 1)
    stat = jnp.where(lane == 0, mean_l, m2_l)
    stat_t = jnp.concatenate([stat, stat], axis=0).T[:8]
    st_send[...] = stat_t
    pl.semaphore_wait(barrier, 15)
    for xx in xpeers:
        send(st_send, st_recv.at[xi], ST, yi, xx)
    perm = one_hot_rows(96, 64, lambda r: jnp.where(
        r % 24 < 16, ((r % 24) // 4) * 16 + (r // 24) * 4 + r % 4,
        jnp.where(r % 24 < 20, yi * 16 + (r // 24) * 4 + r % 4, -1)))
    loaded(FREQ, freq)
    prow = lax.broadcasted_iota(jnp.int32, (24, 128), 0)
    posn = jnp.zeros((24, 128), jnp.int32)
    for r in range(20):
        at = (r // 4) * 16 + xi * 4 + r % 4 if r < 16 else me * 4 + r - 16
        posn = jnp.where(prow == r, lens[at], posn)
    angle = posn.astype(F32) * freq[...]
    table[0] = jnp.cos(angle)
    table[1] = jnp.sin(angle)
    recv(st_recv.at[three], ST)
    parts = [stat_t] + [st_recv[xx] for xx in xpeers]
    means = [p[0:1] for p in parts]
    mu = (means[0] + means[1] + means[2] + means[3]) * 0.25
    m2 = sum([p[1:2] for p in parts]) + wid * sum([(m - mu) * (m - mu) for m in means])
    rstd = lax.rsqrt(m2 * (1.0 / (4 * wid)) + EPS)
    sub = lax.broadcasted_iota(jnp.int32, (128, 128), 0)
    cols_t = jnp.where(sub == 0, mu, rstd).T
    mu_c = cols_t[:rows, 0:1]
    rstd_c = cols_t[:rows, 1:2]
    normed = ((h - mu_c) * rstd_c * ga[...]).astype(BF16)
    n_perm = dot(perm, normed).astype(BF16)

    loaded(WQ, wq)
    loaded(WKV, wkv)
    q_part = dot(n_perm, wq[...])
    kv_part = jnp.concatenate([dot(n_perm, wkv[0]), dot(n_perm, wkv[1])], axis=1)
    prow = lax.broadcasted_iota(jnp.int32, (96, 2 * hd), 0)
    qkv[...] = jnp.where(prow % 24 < 16, q_part, kv_part).reshape(4, 24, 2 * hd)
    for xx in (x2, x3, x1):
        send(qkv.at[xx], qkv_recv.at[xi], QKV, yi, xx)

    for i, xx in enumerate((x1, x3, x2, xi)):
        loaded(WGU + i, wgu.at[xx])
        gup[xx, 0] = dot(normed, wgu[xx, 0])
        gup[xx, 1] = dot(normed, wgu[xx, 1])
        if i < 2:
            send(gup.at[xx], gu_recv.at[i], GU, yi, x1)

    recv(qkv_recv.at[three], QKV)
    tot = ((qkv[xi] + qkv_recv[x1]) + (qkv_recv[x2] + qkv_recv[x3])).astype(BF16).astype(F32)
    half = hd // 2
    cos_a = table[0]
    sin_a = table[1]
    lo0, hi0, lo1, hi1 = [tot[:, i * half:(i + 1) * half] for i in range(4)]
    r0 = (lo0 * cos_a - hi0 * sin_a).astype(BF16)
    r1 = (hi0 * cos_a + lo0 * sin_a).astype(BF16)
    r2 = (lo1 * cos_a - hi1 * sin_a).astype(BF16)
    r3 = (hi1 * cos_a + lo1 * sin_a).astype(BF16)
    kns[:, :half] = r0[16:].astype(F32)
    kns[:, half:] = r1[16:].astype(F32)
    vns[...] = tot[16:, hd:]
    stacked = jnp.concatenate([r0[:16], r1[:16], r2[:16], r3[:16]], axis=0)
    s1 = one_hot_rows(64, 64, lambda r: ((r // 4) % 4) * 16 + (r // 16) * 4 + r % 4)
    q_send[...] = dot(s1, stacked).astype(BF16).reshape(4, 16, 128)
    for yy in ypeers:
        send(q_send.at[yy], q_recv.at[yi], Q, yy, xi)
    q_recv[yi] = q_send[yi]
    kv_out[0] = kns[...]
    kv_out[1] = vns[...]

    recv(gu_recv, GU)
    gux[...] = gup[x2] + gu_recv[1]
    send(gux, gux_recv, GUX, yi, x2)
    recv(q_recv.at[three], Q)
    s2 = one_hot_rows(64, 64, lambda r: ((r // 2) % 4) * 16 + (r % 2) * 8 + (r // 32) * 4 + (r // 8) % 4)
    q_all = dot(s2, q_recv[...].reshape(64, 128))
    qs[...] = jnp.concatenate([q_all[:32], q_all[32:]], axis=1).reshape(4, 8, hd)

    loaded(KEY, kbuf)
    loaded(VAL, vbuf)
    scale = hd ** -0.5
    pos = lax.broadcasted_iota(jnp.int32, (8, seq), 1)

    def scores(j):
        qj = qs[j].astype(BF16)
        for t in range(seq // 256):
            at = pl.ds(t * 256, 256)
            sbuf[j % 2, :, at] = dot_t(qj, kbuf[j, at])

    def mix(j):
        s_new = jnp.sum(qs[j] * kns[j:j + 1, :], axis=1, keepdims=True) * scale
        s = jnp.where(pos < lens[me * 4 + j], sbuf[j % 2] * scale, -jnp.inf)
        top = jnp.maximum(jnp.max(s, axis=1, keepdims=True), s_new)
        w = jnp.exp(s - top)
        w_new = jnp.exp(s_new - top)
        inv = 1.0 / (jnp.sum(w, axis=1, keepdims=True) + w_new)
        prob = (w * inv).astype(BF16)
        p_new = (w_new * inv).astype(BF16).astype(F32)
        os_[j] = dot(prob, vbuf[j]) + p_new * vns[j:j + 1, :]

    def load_embedding(j):
        voc = pl.ds(j * vb, vb)
        load(EK, (emb_hbm.at[voc, pl.ds(0, hd)], kbuf.at[j, pl.ds(0, vb)]))
        load(EV, (emb_hbm.at[voc, pl.ds(hd, hd)], vbuf.at[j, pl.ds(0, vb)]))

    scores(0)
    scores(1)
    mix(0)
    load_embedding(0)
    scores(2)
    mix(1)
    load_embedding(1)
    recv(gux_recv, GUX)
    gu = gup[xi] + gu_recv[0] + gux_recv[...]
    gate = gu[0].astype(BF16).astype(F32)
    up_val = gu[1].astype(BF16).astype(F32)
    m_all[xi] = (gate * jax.nn.sigmoid(gate) * up_val).astype(BF16)
    for xx in (x2, x3, x1):
        send(m_all.at[xi], m_all.at[xi], M, yi, xx)
    scores(3)
    mix(2)
    load_embedding(2)
    mix(3)
    load_embedding(3)

    o_bf = os_[...].reshape(32, hd).astype(BF16)
    s3 = one_hot_rows(64, 64, lambda r: ((r // 4) % 2) * 32 + (r % 4) * 8 + (r // 16) * 2 + (r // 8) % 2)
    o_send[...] = dot(s3, jnp.concatenate([o_bf[:, :half], o_bf[:, half:]], axis=0)).astype(BF16).reshape(4, 16, 128)
    for yy in ypeers:
        for xx in (x3, x2, x1, xi):
            send(o_send.at[yy], o_recv.at[me], O, yy, xx)
    for xx in xpeers:
        send(o_send.at[yi], o_recv.at[me], O, yi, xx)
    o_recv[me] = o_send[yi]

    loaded(WD, wd)
    loaded(WO, wo)
    loaded(GF, gf)
    recv(m_all.at[three], M)
    mdown[...] = sum([dot(m_all[i], wd[pl.ds(i * ffc, ffc)]) for i in range(4)])
    s4 = one_hot_rows(256, 256, lambda r: ((r % 64) // 4) * 16 + (r // 64) * 4 + r % 4)
    recv(o_recv.at[most], O)
    a_all = dot(s4, o_recv[...].reshape(256, 128)).astype(BF16)
    attn = jnp.concatenate([a_all[i * 64:(i + 1) * 64] for i in range(4)], axis=1)
    bpart[...] = (dot(attn, wo[...]) + mdown[...]).reshape(4, 16, wid)
    for yy in (ypeers[1], ypeers[0], ypeers[2]):
        send(bpart.at[yy], b_recv.at[yi], B, yy, xi)
    res = hid[pl.ds(pl.multiple_of(yi * 16, 16), 16), :].astype(F32)
    recv(b_recv.at[three], B)
    res = res + ((bpart[yi] + b_recv[ypeers[0]]) + (b_recv[ypeers[1]] + b_recv[ypeers[2]]))

    mean_l = jnp.sum(res, axis=1, keepdims=True) * (1.0 / wid)
    dev = res - mean_l
    m2_l = jnp.sum(dev * dev, axis=1, keepdims=True)
    lane = lax.broadcasted_iota(jnp.int32, (16, 128), 1)
    s2_send[...] = jnp.where(lane < 64, mean_l, m2_l)
    for xx in xpeers:
        send(s2_send, s2_recv.at[xi], S2, yi, xx)
    recv(s2_recv.at[three], S2)
    parts = [s2_recv[xx] for xx in xpeers]
    means = [mean_l] + [p[:, 0:1] for p in parts]
    mu = (means[0] + means[1] + means[2] + means[3]) * 0.25
    m2 = m2_l + sum([p[:, 64:65] for p in parts]) + wid * sum([(m - mu) * (m - mu) for m in means])
    rstd = lax.rsqrt(m2 * (1.0 / (4 * wid)) + EPS)
    f_own = ((res - mu) * rstd * gf[...]).astype(BF16)
    fbuf[yi] = f_own
    for yy in ypeers:
        send(fbuf.at[yi], fbuf.at[yi], FN, yy, xi)
    loaded(EK, kbuf.at[:, pl.ds(0, vb)])
    loaded(EV, vbuf.at[:, pl.ds(0, vb)])

    def logit_part(f, xx, c0, cn):
        voc = pl.ds(c0, cn)
        return dot_t(f[:, :hd], kbuf[xx, voc]) + dot_t(f[:, hd:], vbuf[xx, voc])

    def cross(i, at):
        recv_chunk(lrecv1.at[at], l1_sem.at[i])
        hold[at] = hold[at] + lrecv1[at]
        send(hold.at[at], xrecv.at[at], LX, yi, x2, lx_sem.at[i])

    def cross_blocks(f, slots, chunks, first):
        n = f.shape[0] // 16
        prev = None
        for i, (c0, cn) in enumerate(chunks):
            at = (slots, slice(None), pl.ds(c0, cn))
            lsend1[at] = logit_part(f, x3, c0, cn).reshape(n, 16, cn)
            send(lsend1.at[at], lrecv1.at[at], L1, yi, x1, l1_sem.at[first + i])
            hold[at] = logit_part(f, x2, c0, cn).reshape(n, 16, cn)
            if prev is not None:
                cross(*prev)
            prev = (first + i, at)
        cross(*prev)

    slot_a = pl.ds(0, 1)
    slot_b = pl.ds(1, 3)
    na = len(chunks_a)
    cross_blocks(f_own, slot_a, chunks_a, 0)
    recv(fbuf.at[three], FN)
    f_rest = jnp.concatenate([fbuf[yy] for yy in ypeers], axis=0)
    cross_blocks(f_rest, slot_b, chunks_b, na)
    f_all = jnp.concatenate([f_own, f_rest], axis=0)
    for i, (c0, cn) in enumerate(chunks_c):
        at = (slice(None), slice(None), pl.ds(c0, cn))
        lsend2[at] = logit_part(f_all, x1, c0, cn).reshape(4, 16, cn)
        send(lsend2.at[at], lrecv2.at[at], L2, yi, x1, l2_sem.at[i])
        own[at] = logit_part(f_all, xi, c0, cn).reshape(4, 16, cn)
    recv_chunk(lrecv2, l2_sem.at[0]) if len(chunks_c) == 1 else [
        recv_chunk(lrecv2.at[:, :, pl.ds(c0, cn)], l2_sem.at[i]) for i, (c0, cn) in enumerate(chunks_c)]
    tops, totals = {}, {}
    for d in range(4):
        tops[d] = jnp.full((16, 1), -jnp.inf, F32)
        totals[d] = jnp.zeros((16, 1), F32)
    for chunks, slots, ds, first in ((chunks_a, slot_a, (0,), 0), (chunks_b, slot_b, (1, 2, 3), na)):
        for i, (c0, cn) in enumerate(chunks):
            recv_chunk(xrecv.at[slots, :, pl.ds(c0, cn)], lx_sem.at[first + i])
            cs = pl.ds(c0, cn)
            for d in ds:
                row = pl.ds(pl.multiple_of(((yi + d) % 4) * 16, 16), 16)
                z = own[d, :, cs] + lrecv2[d, :, cs] + xrecv[d, :, cs]
                if c0 + cn > vb:
                    z_out[row, c0:vb] = z[:, :vb - c0]
                    z = jnp.where(lax.broadcasted_iota(jnp.int32, (16, cn), 1) < vb - c0, z, -jnp.inf)
                else:
                    z_out[row, cs] = z
                m_new = jnp.maximum(tops[d], jnp.max(z, axis=1, keepdims=True))
                totals[d] = totals[d] * jnp.exp(tops[d] - m_new) + jnp.sum(jnp.exp(z - m_new), axis=1, keepdims=True)
                tops[d] = m_new
    lane = lax.broadcasted_iota(jnp.int32, (16, 128), 1)
    for d in range(4):
        lcol[(yi + d) % 4] = jnp.where(lane == 0, tops[d], totals[d])

    stat = lcol[...].reshape(rows, 128)
    mine = jnp.concatenate([stat, stat], axis=0).T[0:2]
    l_send[...] = mine
    for yy in ypeers:
        for xx in (x3, x2, x1, xi):
            send(l_send, l_recv.at[me], LSE, yy, xx)
    for xx in xpeers:
        send(l_send, l_recv.at[me], LSE, yi, xx)
    l_recv[me] = mine
    sent(st_recv.at[three], ST)
    sent(qkv.at[three], QKV)
    sent(q_send.at[three], Q)
    sent(gu_recv, GU)
    sent(gux, GUX)
    sent(m_all.at[three], M)
    sent(o_recv.at[most], O)
    sent(bpart.at[three], B)
    sent(s2_recv.at[three], S2)
    sent(fbuf.at[three], FN)
    sent(lsend1, L1)
    sent(hold, LX)
    sent(lsend2, L2)
    recv(l_recv.at[most], LSE)
    tops = [l_recv[i, 0:1, :] for i in range(16)]
    top = functools.reduce(jnp.maximum, tops)
    total = sum([l_recv[i, 1:2, :] * jnp.exp(tops[i] - top) for i in range(16)])
    log_norm = top + jnp.log(total)
    lr_out[...] = log_norm[:, :rows]
    ln_out[...] = jnp.broadcast_to(log_norm, (128, 128)).T[:rows, 0:1]
    sent(l_recv.at[most], LSE)


def finish_kernel(own_rows, kv, z, ln, lr, k_out, v_out, lp_out, ln_out, k_s, v_s, lp_s, sem):
    k_s[...] = kv[0].astype(BF16)[:own_rows]
    v_s[...] = kv[1].astype(BF16)[:own_rows]
    copies = [pltpu.make_async_copy(k_s, k_out, sem.at[0]), pltpu.make_async_copy(v_s, v_out, sem.at[1]),
              pltpu.make_async_copy(lr, ln_out, sem.at[2])]
    for cp in copies:
        cp.start()
    for i in range(z.shape[0] // 8):
        at = pl.ds(i * 8, 8)
        lp_s[at] = z[at] - ln[at]
        copies.append(pltpu.make_async_copy(lp_s.at[at], lp_out.at[at], sem.at[3 + i]))
        copies[-1].start()
    for cp in copies:
        cp.wait()


def solution(mesh):
    row_spec = P(("dp", "yax", "xax"))

    def local_step(hidden, cache_len, k_cache, v_cache, g_attn, w_query, w_key, w_value,
                   w_gate, w_up, w_out, w_down, g_final, embedding):
        rows, wid = hidden.shape
        own_rows, seq, hd = k_cache.shape
        ffc = w_gate.shape[1] // 4
        vb = embedding.shape[0] // 4
        half_dim = hd // 2
        inv_freq = ROPE_BASE ** (-(jnp.arange(half_dim, dtype=jnp.float32) * 2.0) / hd)
        vbp = -(-vb // 128) * 128
        def cut(step):
            return [(c, min(step, vbp - c)) for c in range(0, vbp, step)]

        chunks_a, chunks_b, chunks_c = cut(1024), cut(512), cut(1024)
        nx, nc = len(chunks_a) + len(chunks_b), len(chunks_c)
        sizes = (rows, wid, seq, hd, ffc, vb, chunks_a, chunks_b, chunks_c)
        any_spec = pl.BlockSpec(memory_space=pltpu.HBM)
        vmem = pl.BlockSpec(memory_space=pltpu.VMEM)
        v = pltpu.VMEM
        dma = pltpu.SemaphoreType.DMA
        scratch = [
            v((rows, wid), BF16), v((1, hd // 2), F32), v((2, 24, hd // 2), F32), v((1, wid), F32), v((1, wid), F32),
            v((4, seq, hd), BF16), v((4, seq, hd), BF16),
            v((wid, 2 * hd), BF16), v((2, wid, hd), BF16), v((4, 2, wid, ffc), BF16),
            v((2 * hd, wid), BF16), v((4 * ffc, wid), BF16),
            v((8, 128), F32), v((4, 8, 128), F32), v((4, 24, 2 * hd), F32), v((4, 24, 2 * hd), F32),
            v((4, 16, 128), BF16), v((4, 16, 128), BF16), v((4, 8, hd), F32), v((8, hd), F32), v((8, hd), F32),
            v((4, 8, hd), F32), v((2, 8, seq), F32), v((4, 16, 128), BF16), v((16, 16, 128), BF16),
            v((4, 2, rows, ffc), F32), v((2, 2, rows, ffc), F32), v((2, rows, ffc), F32), v((2, rows, ffc), F32),
            v((4, rows, ffc), BF16), v((rows, wid), F32), v((4, 16, wid), F32), v((4, 16, wid), F32),
            v((16, 128), F32), v((4, 16, 128), F32), v((4, 16, wid), BF16),
            v((4, 16, vbp), F32), v((4, 16, vbp), F32), v((4, 16, vbp), F32), v((4, 16, vbp), F32),
            v((4, 16, vbp), F32), v((4, 16, vbp), F32), v((4, 16, vbp), F32), v((4, 16, 128), F32),
            v((2, 128), F32), v((16, 2, 128), F32),
            dma((16,)), dma((14,)), dma((11,)), dma((nx,)), dma((nx,)), dma((nc,)),
        ]
        kv, z, ln, lr = pl.pallas_call(
            functools.partial(step_kernel, sizes),
            name="decode_step",
            out_shape=(v((2, 8, hd), F32), v((rows, vb), F32), v((rows, 1), F32), v((1, rows), F32)),
            in_specs=[pl.BlockSpec(memory_space=pltpu.SMEM)] + [any_spec] * 14,
            out_specs=(vmem, vmem, vmem, vmem),
            scratch_shapes=scratch,
            compiler_params=pltpu.CompilerParams(collective_id=0, has_side_effects=True,
                                                 vmem_limit_bytes=67043328 - 900 * 1024),
        )(cache_len, hidden, inv_freq.reshape(1, half_dim), k_cache, v_cache, g_attn.reshape(1, wid), w_query, w_key, w_value,
          w_gate, w_up, w_out, w_down, g_final.reshape(1, wid), embedding)
        k_new, v_new, log_probs, log_norm = pl.pallas_call(
            functools.partial(finish_kernel, own_rows),
            name="finish_step",
            out_shape=(jax.ShapeDtypeStruct((own_rows, hd), BF16), jax.ShapeDtypeStruct((own_rows, hd), BF16),
                       jax.ShapeDtypeStruct((rows, vb), F32), jax.ShapeDtypeStruct((1, rows), F32)),
            in_specs=[vmem] * 4,
            out_specs=(any_spec,) * 4,
            scratch_shapes=[v((own_rows, hd), BF16), v((own_rows, hd), BF16), v((rows, vb), F32), dma((11,))],
            compiler_params=pltpu.CompilerParams(vmem_limit_bytes=4 * 1024 * 1024),
        )(kv, z, ln, lr)
        return k_new, v_new, log_probs, log_norm[0]

    in_specs = (P("dp", "xax"), P("dp"), row_spec, row_spec, P("xax"), P("xax", "yax"),
                P("xax", None), P("xax", None), P("xax", "yax"), P("xax", "yax"),
                P("yax", "xax"), P("yax", "xax"), P("xax"), P("yax", "xax"))
    out_specs = (row_spec, row_spec, P("dp", ("yax", "xax")), P("dp"))
    return jax.shard_map(local_step, mesh=mesh, in_specs=in_specs, out_specs=out_specs, check_vma=False)
```

time: 82.5 us -> 66.3 us (0.80)
  Pallas kernels: 74.3 us -> 65 us
  local copies, waits for them, and re-layouts: 3.37 us -> 0 us
  other arithmetic: 3.86 us -> 0.53 us
    pallas_call x1, Pallas kernels: 74.3 us -> 63.9 us  [local_step(): pl.pallas_call(functools.partial(step_kernel, sizes), name='decode_step',...]
    unnamed x4 -> x0, local copies, waits for them, and re-layouts: 2.5 us -> none
    sub x1 -> x0, other arithmetic: 2.16 us -> none  [local_step(): return (k_new, v_new, z - ln, ln[:, 0])]
    pallas_call x0 -> x1, Pallas kernels: none -> 1.06 us  [local_step(): pl.pallas_call(functools.partial(finish_kernel, own_rows), name='finish_s...]
    pallas_call x1 -> x0, other arithmetic: 0.87 us -> none  [local_step(): pl.pallas_call(functools.partial(step_kernel, sizes), name='decode_step',...]
where the time goes in v2:
time: 66.3 us; the launch traced here: 66.1 us
  Pallas kernels  65 us (98%)
    pallas_call x1, Pallas kernels, local_step(): pl.pallas_call(functools.partial(step_kernel, sizes), name='decode_step',...  63.9 us

profile of v2, /device:TPU:0, one launch (start us, length us, event | category | flops | bytes accessed | tf_op | source)
XLA Modules:
  0.0 66.1 jit_solution(6461076276430826577)
XLA Ops:
  0.6 0.5 multiply_power_fusion.freq_hbm
  1.2 63.9 %decode_step.1 = (f32[2,8,256]{2,1,0:T(8,128)S(1)}, f32[64,3144]{1,0:T(8,128)S(1)}, f32[64,1]{1,0:T(8,128)S(1)}, f32[1,64]{1,0:T(1,128)S(1)}) custom-call(s32[64]{0:T(128)} %lens.1, bf16[64,512]{1,0:T(8,128)(2,1)} %hidden_hbm.1, f32[1,128]{1,0:T(1,128)} %multiply_power_fusion.freq_hbm, bf16[4,8192,256]{2,1,0:T(8,128)(2,1)} %k_hbm.1, ...), custom_call_target="tpu_custom_call" | custom-call | tf_op jit(solution)/shard_map/decode_step/pallas_call | solution.py:420
  65.1 1.1 %finish_step.1 = (bf16[4,256]{1,0:T(4,128)(2,1)}, bf16[4,256]{1,0:T(4,128)(2,1)}, f32[64,3144]{1,0:T(8,128)}, f32[1,64]{1,0:T(1,128)}) custom-call(f32[2,8,256]{2,1,0:T(8,128)S(1)} %get-tuple-element.12.kv, f32[64,3144]{1,0:T(8,128)S(1)} %get-tuple-element.13.z, f32[64,1]{1,0:T(8,128)S(1)} %get-tuple-element.14.ln, f32[1,64]{1,0:T(1,128)S(1)} %get-tuple-element.15.lr), custom_call_target="tpu_custom_call" | custom-call | tf_op jit(solution)/shard_map/finish_step/pallas_call | solution.py:431

commit v3 on v2

--- a/solution.py
+++ b/solution.py
@@ -2,6 +2,7 @@
 
 import jax
 import jax.numpy as jnp
+import numpy as np
 from jax import lax
 from jax.experimental import pallas as pl
 from jax.experimental.pallas import tpu as pltpu
@@ -32,7 +33,7 @@
                 lens, hidden_hbm, freq_hbm, k_hbm, v_hbm, ga_hbm, wq_hbm, wk_hbm, wv_hbm, wg_hbm, wu_hbm,
                 wo_hbm, wd_hbm, gf_hbm, emb_hbm,
                 kv_out, z_out, ln_out, lr_out,
-                hid, freq, table, ga, gf, kbuf, vbuf, wq, wkv, wgu, wo, wd,
+                hid, freq, table, ga, gf, kb0, kb1, kb2, kb3, kb4, vbuf, wq, wkv, wgu, wo, wd,
                 st_send, st_recv, qkv, qkv_recv, q_send, q_recv, qs, kns, vns, os_, sbuf, o_send, o_recv,
                 gup, gu_recv, gux, gux_recv, m_all, mdown, bpart, b_recv, s2_send, s2_recv, fbuf,
                 lsend1, lrecv1, hold, xrecv, lsend2, lrecv2, own, lcol, l_send, l_recv,
@@ -54,7 +55,8 @@
     def loaded(i, dst):
         pltpu.make_async_copy(dst, dst, ld_sem.at[i]).wait()
 
-    HID, GA, FREQ, WQ, WKV, WGU, WD, WO, GF, KEY, VAL, EK, EV = 0, 1, 2, 3, 4, 5, 9, 10, 11, 12, 13, 14, 15
+    HID, GA, FREQ, WQ, WKV, WGU, WD, WO, GF, KEY, VAL, EMB = 0, 1, 2, 3, 4, 5, 9, 10, 11, 12, 16, 20
+    kb = (kb0, kb1, kb2, kb3, kb4)
     load(HID, (hidden_hbm, hid))
     load(GA, (ga_hbm, ga))
     barrier = pltpu.get_barrier_semaphore()
@@ -66,16 +68,19 @@
     load(FREQ, (freq_hbm, freq))
     load(WQ, (wq_hbm, wq))
     load(WKV, (wk_hbm, wkv.at[0]), (wv_hbm, wkv.at[1]))
+    load(KEY, (k_hbm.at[0], kb[1]))
     for i, xx in enumerate((x1, x3, x2, xi)):
         cols = pl.ds(pl.multiple_of(xx * ffc, ffc), ffc)
         load(WGU + i, (wg_hbm.at[:, cols], wgu.at[xx, 0]), (wu_hbm.at[:, cols], wgu.at[xx, 1]))
-    load(KEY, *[(k_hbm.at[j], kbuf.at[j]) for j in range(4)])
-    load(VAL, *[(v_hbm.at[j], vbuf.at[j]) for j in range(4)])
+    for j in range(1, 4):
+        load(KEY + j, (k_hbm.at[j], kb[j + 1]))
+    for j in range(4):
+        load(VAL + j, (v_hbm.at[j], vbuf.at[j]))
     load(WD, (wd_hbm, wd))
     load(WO, (wo_hbm, wo))
     load(GF, (gf_hbm, gf))
 
-    ST, QKV, Q, GU, GUX, M, O, B, S2, FN, LSE, L1, LX, L2 = range(14)
+    ST, QP, KVP, Q, GU, GUX, M, O1, O2, B, S2, FN, LSE, L1, LX, L2 = range(16)
 
     def send(src, dst, i, yy, xx, rsem=None):
         pltpu.make_async_remote_copy(src_ref=src, dst_ref=dst, send_sem=snd_sem.at[i],
@@ -93,6 +98,16 @@
 
     three = pl.ds(0, 3)
     most = pl.ds(0, 15)
+
+    def transpose_keys(j):
+        loaded(KEY + j, kb[j + 1])
+
+        def one(t, carry):
+            at = pl.ds(pl.multiple_of(t * 256, 256), 256)
+            kb[j][at] = kb[j + 1][at].T
+            return carry
+
+        lax.fori_loop(0, seq // 256, one, 0, unroll=8)
 
     loaded(HID, hid)
     loaded(GA, ga)
@@ -119,6 +134,7 @@
     angle = posn.astype(F32) * freq[...]
     table[0] = jnp.cos(angle)
     table[1] = jnp.sin(angle)
+    transpose_keys(0)
     recv(st_recv.at[three], ST)
     parts = [stat_t] + [st_recv[xx] for xx in xpeers]
     means = [p[0:1] for p in parts]
@@ -138,8 +154,11 @@
     kv_part = jnp.concatenate([dot(n_perm, wkv[0]), dot(n_perm, wkv[1])], axis=1)
     prow = lax.broadcasted_iota(jnp.int32, (96, 2 * hd), 0)
     qkv[...] = jnp.where(prow % 24 < 16, q_part, kv_part).reshape(4, 24, 2 * hd)
+    q_rows, kv_rows = pl.ds(0, 16), pl.ds(16, 8)
     for xx in (x2, x3, x1):
-        send(qkv.at[xx], qkv_recv.at[xi], QKV, yi, xx)
+        send(qkv.at[xx, q_rows], qkv_recv.at[xi, q_rows], QP, yi, xx)
+    for xx in (x2, x3, x1):
+        send(qkv.at[xx, kv_rows], qkv_recv.at[xi, kv_rows], KVP, yi, xx)
 
     for i, xx in enumerate((x1, x3, x2, xi)):
         loaded(WGU + i, wgu.at[xx])
@@ -148,38 +167,48 @@
         if i < 2:
             send(gup.at[xx], gu_recv.at[i], GU, yi, x1)
 
-    recv(qkv_recv.at[three], QKV)
-    tot = ((qkv[xi] + qkv_recv[x1]) + (qkv_recv[x2] + qkv_recv[x3])).astype(BF16).astype(F32)
+    transpose_keys(1)
+    transpose_keys(2)
     half = hd // 2
-    cos_a = table[0]
-    sin_a = table[1]
+    recv(qkv_recv.at[three, q_rows], QP)
+
+    def total(at):
+        return ((qkv[xi, at] + qkv_recv[x1, at]) + (qkv_recv[x2, at] + qkv_recv[x3, at])).astype(BF16).astype(F32)
+
+    def rotary(lo, hi, at):
+        cos_a, sin_a = table[0, at], table[1, at]
+        return (lo * cos_a - hi * sin_a).astype(BF16), (hi * cos_a + lo * sin_a).astype(BF16)
+
+    tot = total(q_rows)
     lo0, hi0, lo1, hi1 = [tot[:, i * half:(i + 1) * half] for i in range(4)]
-    r0 = (lo0 * cos_a - hi0 * sin_a).astype(BF16)
-    r1 = (hi0 * cos_a + lo0 * sin_a).astype(BF16)
-    r2 = (lo1 * cos_a - hi1 * sin_a).astype(BF16)
-    r3 = (hi1 * cos_a + lo1 * sin_a).astype(BF16)
-    kns[:, :half] = r0[16:].astype(F32)
-    kns[:, half:] = r1[16:].astype(F32)
-    vns[...] = tot[16:, hd:]
-    stacked = jnp.concatenate([r0[:16], r1[:16], r2[:16], r3[:16]], axis=0)
+    r0, r1 = rotary(lo0, hi0, q_rows)
+    r2, r3 = rotary(lo1, hi1, q_rows)
+    stacked = jnp.concatenate([r0, r1, r2, r3], axis=0)
     s1 = one_hot_rows(64, 64, lambda r: ((r // 4) % 4) * 16 + (r // 16) * 4 + r % 4)
     q_send[...] = dot(s1, stacked).astype(BF16).reshape(4, 16, 128)
     for yy in ypeers:
         send(q_send.at[yy], q_recv.at[yi], Q, yy, xi)
     q_recv[yi] = q_send[yi]
+    recv(qkv_recv.at[three, kv_rows], KVP)
+    tot = total(kv_rows)
+    r0, r1 = rotary(tot[:, :half], tot[:, half:hd], kv_rows)
+    kns[:, :half] = r0.astype(F32)
+    kns[:, half:] = r1.astype(F32)
+    vns[...] = tot[:, hd:]
     kv_out[0] = kns[...]
     kv_out[1] = vns[...]
 
     recv(gu_recv, GU)
     gux[...] = gup[x2] + gu_recv[1]
     send(gux, gux_recv, GUX, yi, x2)
+    transpose_keys(3)
     recv(q_recv.at[three], Q)
     s2 = one_hot_rows(64, 64, lambda r: ((r // 2) % 4) * 16 + (r % 2) * 8 + (r // 32) * 4 + (r // 8) % 4)
     q_all = dot(s2, q_recv[...].reshape(64, 128))
     qs[...] = jnp.concatenate([q_all[:32], q_all[32:]], axis=1).reshape(4, 8, hd)
 
-    loaded(KEY, kbuf)
-    loaded(VAL, vbuf)
+    for j in range(4):
+        loaded(VAL + j, vbuf.at[j])
     scale = hd ** -0.5
     pos = lax.broadcasted_iota(jnp.int32, (8, seq), 1)
 
@@ -187,7 +216,7 @@
         qj = qs[j].astype(BF16)
         for t in range(seq // 256):
             at = pl.ds(t * 256, 256)
-            sbuf[j % 2, :, at] = dot_t(qj, kbuf[j, at])
+            sbuf[j % 2, :, at] = dot(qj, kb[j][at])
 
     def mix(j):
         s_new = jnp.sum(qs[j] * kns[j:j + 1, :], axis=1, keepdims=True) * scale
@@ -198,20 +227,30 @@
         inv = 1.0 / (jnp.sum(w, axis=1, keepdims=True) + w_new)
         prob = (w * inv).astype(BF16)
         p_new = (w_new * inv).astype(BF16).astype(F32)
-        os_[j] = dot(prob, vbuf[j]) + p_new * vns[j:j + 1, :]
-
-    def load_embedding(j):
-        voc = pl.ds(j * vb, vb)
-        load(EK, (emb_hbm.at[voc, pl.ds(0, hd)], kbuf.at[j, pl.ds(0, vb)]))
-        load(EV, (emb_hbm.at[voc, pl.ds(hd, hd)], vbuf.at[j, pl.ds(0, vb)]))
+        hs = seq // 2
+        acc = dot(prob[:, :hs], vbuf[j, :hs]) + dot(prob[:, hs:], vbuf[j, hs:])
+        os_[j] = acc + p_new * vns[j:j + 1, :]
+
+    s3 = one_hot_rows(32, 32, lambda r: ((r // 2) % 2) * 16 + (r % 2) * 8 + (r // 8) * 2 + (r // 4) % 2)
+
+    def send_outputs(pair, i):
+        o_bf = os_[2 * pair:2 * pair + 2].reshape(16, hd).astype(BF16)
+        o_rows = dot(s3, jnp.concatenate([o_bf[:, :half], o_bf[:, half:]], axis=0))
+        o_send[pair] = o_rows.reshape(4, 8, 128).astype(BF16)
+        for yy in ypeers:
+            for xx in (x3, x2, x1, xi):
+                send(o_send.at[pair, yy], o_recv.at[pair, me], i, yy, xx)
+        for xx in xpeers:
+            send(o_send.at[pair, yi], o_recv.at[pair, me], i, yi, xx)
+        o_recv[pair, me] = o_send[pair, yi]
 
     scores(0)
     scores(1)
     mix(0)
-    load_embedding(0)
     scores(2)
     mix(1)
-    load_embedding(1)
+    scores(3)
+    mix(2)
     recv(gux_recv, GUX)
     gu = gup[xi] + gu_recv[0] + gux_recv[...]
     gate = gu[0].astype(BF16).astype(F32)
@@ -219,30 +258,23 @@
     m_all[xi] = (gate * jax.nn.sigmoid(gate) * up_val).astype(BF16)
     for xx in (x2, x3, x1):
         send(m_all.at[xi], m_all.at[xi], M, yi, xx)
-    scores(3)
-    mix(2)
-    load_embedding(2)
+    send_outputs(0, O1)
     mix(3)
-    load_embedding(3)
-
-    o_bf = os_[...].reshape(32, hd).astype(BF16)
-    s3 = one_hot_rows(64, 64, lambda r: ((r // 4) % 2) * 32 + (r % 4) * 8 + (r // 16) * 2 + (r // 8) % 2)
-    o_send[...] = dot(s3, jnp.concatenate([o_bf[:, :half], o_bf[:, half:]], axis=0)).astype(BF16).reshape(4, 16, 128)
-    for yy in ypeers:
-        for xx in (x3, x2, x1, xi):
-            send(o_send.at[yy], o_recv.at[me], O, yy, xx)
-    for xx in xpeers:
-        send(o_send.at[yi], o_recv.at[me], O, yi, xx)
-    o_recv[me] = o_send[yi]
-
+    send_outputs(1, O2)
+    for j in range(4):
+        voc = pl.ds(j * vb, vb)
+        load(EMB, (emb_hbm.at[voc, pl.ds(0, hd)], vbuf.at[j, pl.ds(0, vb)]),
+             (emb_hbm.at[voc, pl.ds(hd, hd)], vbuf.at[j, pl.ds(seq // 2, vb)]))
     loaded(WD, wd)
     loaded(WO, wo)
     loaded(GF, gf)
     recv(m_all.at[three], M)
     mdown[...] = sum([dot(m_all[i], wd[pl.ds(i * ffc, ffc)]) for i in range(4)])
-    s4 = one_hot_rows(256, 256, lambda r: ((r % 64) // 4) * 16 + (r // 64) * 4 + r % 4)
-    recv(o_recv.at[most], O)
-    a_all = dot(s4, o_recv[...].reshape(256, 128)).astype(BF16)
+    s4 = one_hot_rows(256, 256, lambda r: ((r // 2) % 2) * 128 + ((r % 64) // 4) * 8 + (r // 64) * 2 + r % 2)
+    recv(o_recv.at[0, most], O1)
+    recv(o_recv.at[1, most], O2)
+    o_rows = jnp.concatenate([o_recv[pair, i].astype(F32) for pair in range(2) for i in range(16)], axis=0)
+    a_all = dot(s4, o_rows.astype(BF16)).astype(BF16)
     attn = jnp.concatenate([a_all[i * 64:(i + 1) * 64] for i in range(4)], axis=1)
     bpart[...] = (dot(attn, wo[...]) + mdown[...]).reshape(4, 16, wid)
     for yy in (ypeers[1], ypeers[0], ypeers[2]):
@@ -268,12 +300,10 @@
     fbuf[yi] = f_own
     for yy in ypeers:
         send(fbuf.at[yi], fbuf.at[yi], FN, yy, xi)
-    loaded(EK, kbuf.at[:, pl.ds(0, vb)])
-    loaded(EV, vbuf.at[:, pl.ds(0, vb)])
+    loaded(EMB, vbuf.at[:, pl.ds(0, 2 * vb)])
 
     def logit_part(f, xx, c0, cn):
-        voc = pl.ds(c0, cn)
-        return dot_t(f[:, :hd], kbuf[xx, voc]) + dot_t(f[:, hd:], vbuf[xx, voc])
+        return dot_t(f[:, :hd], vbuf[xx, pl.ds(c0, cn)]) + dot_t(f[:, hd:], vbuf[xx, pl.ds(seq // 2 + c0, cn)])
 
     def cross(i, at):
         recv_chunk(lrecv1.at[at], l1_sem.at[i])
@@ -341,12 +371,14 @@
         send(l_send, l_recv.at[me], LSE, yi, xx)
     l_recv[me] = mine
     sent(st_recv.at[three], ST)
-    sent(qkv.at[three], QKV)
+    sent(qkv.at[three, q_rows], QP)
+    sent(qkv.at[three, kv_rows], KVP)
     sent(q_send.at[three], Q)
     sent(gu_recv, GU)
     sent(gux, GUX)
     sent(m_all.at[three], M)
-    sent(o_recv.at[most], O)
+    sent(o_recv.at[0, most], O1)
+    sent(o_recv.at[1, most], O2)
     sent(bpart.at[three], B)
     sent(s2_recv.at[three], S2)
     sent(fbuf.at[three], FN)
@@ -388,13 +420,12 @@
         own_rows, seq, hd = k_cache.shape
         ffc = w_gate.shape[1] // 4
         vb = embedding.shape[0] // 4
-        half_dim = hd // 2
-        inv_freq = ROPE_BASE ** (-(jnp.arange(half_dim, dtype=jnp.float32) * 2.0) / hd)
+        inv_freq = np.power(ROPE_BASE, -2.0 * np.arange(hd // 2) / hd).astype(np.float32).reshape(1, hd // 2)
         vbp = -(-vb // 128) * 128
         def cut(step):
             return [(c, min(step, vbp - c)) for c in range(0, vbp, step)]
 
-        chunks_a, chunks_b, chunks_c = cut(1024), cut(512), cut(1024)
+        chunks_a, chunks_b, chunks_c = cut(512), cut(512), cut(1024)
         nx, nc = len(chunks_a) + len(chunks_b), len(chunks_c)
         sizes = (rows, wid, seq, hd, ffc, vb, chunks_a, chunks_b, chunks_c)
         any_spec = pl.BlockSpec(memory_space=pltpu.HBM)
@@ -403,19 +434,19 @@
         dma = pltpu.SemaphoreType.DMA
         scratch = [
             v((rows, wid), BF16), v((1, hd // 2), F32), v((2, 24, hd // 2), F32), v((1, wid), F32), v((1, wid), F32),
-            v((4, seq, hd), BF16), v((4, seq, hd), BF16),
+            *[v((seq, hd), BF16)] * 5, v((4, seq, hd), BF16),
             v((wid, 2 * hd), BF16), v((2, wid, hd), BF16), v((4, 2, wid, ffc), BF16),
             v((2 * hd, wid), BF16), v((4 * ffc, wid), BF16),
             v((8, 128), F32), v((4, 8, 128), F32), v((4, 24, 2 * hd), F32), v((4, 24, 2 * hd), F32),
             v((4, 16, 128), BF16), v((4, 16, 128), BF16), v((4, 8, hd), F32), v((8, hd), F32), v((8, hd), F32),
-            v((4, 8, hd), F32), v((2, 8, seq), F32), v((4, 16, 128), BF16), v((16, 16, 128), BF16),
+            v((4, 8, hd), F32), v((2, 8, seq), F32), v((2, 4, 8, 128), BF16), v((2, 16, 8, 128), BF16),
             v((4, 2, rows, ffc), F32), v((2, 2, rows, ffc), F32), v((2, rows, ffc), F32), v((2, rows, ffc), F32),
             v((4, rows, ffc), BF16), v((rows, wid), F32), v((4, 16, wid), F32), v((4, 16, wid), F32),
             v((16, 128), F32), v((4, 16, 128), F32), v((4, 16, wid), BF16),
             v((4, 16, vbp), F32), v((4, 16, vbp), F32), v((4, 16, vbp), F32), v((4, 16, vbp), F32),
             v((4, 16, vbp), F32), v((4, 16, vbp), F32), v((4, 16, vbp), F32), v((4, 16, 128), F32),
             v((2, 128), F32), v((16, 2, 128), F32),
-            dma((16,)), dma((14,)), dma((11,)), dma((nx,)), dma((nx,)), dma((nc,)),
+            dma((21,)), dma((16,)), dma((13,)), dma((nx,)), dma((nx,)), dma((nc,)),
         ]
         kv, z, ln, lr = pl.pallas_call(
             functools.partial(step_kernel, sizes),
@@ -426,7 +457,7 @@
             scratch_shapes=scratch,
             compiler_params=pltpu.CompilerParams(collective_id=0, has_side_effects=True,
                                                  vmem_limit_bytes=67043328 - 900 * 1024),
-        )(cache_len, hidden, inv_freq.reshape(1, half_dim), k_cache, v_cache, g_attn.reshape(1, wid), w_query, w_key, w_value,
+        )(cache_len, hidden, jnp.asarray(inv_freq), k_cache, v_cache, g_attn.reshape(1, wid), w_query, w_key, w_value,
           w_gate, w_up, w_out, w_down, g_final.reshape(1, wid), embedding)
         k_new, v_new, log_probs, log_norm = pl.pallas_call(
             functools.partial(finish_kernel, own_rows),

time: 66.3 us -> 63.4 us (0.956)
  Pallas kernels: 65 us -> 62.6 us
    pallas_call x1, Pallas kernels: 63.9 us -> 61.6 us  [local_step(): pl.pallas_call(functools.partial(step_kernel, sizes), name='decode_step',...]
where the time goes in v3:
time: 63.4 us; the launch traced here: 63.3 us
  Pallas kernels  62.6 us (99%)
  between operations  0.64 us (1%)
    pallas_call x1, Pallas kernels, local_step(): pl.pallas_call(functools.partial(step_kernel, sizes), name='decode_step',...  61.6 us

profile of v3, /device:TPU:0, one launch (start us, length us, event | category | flops | bytes accessed | tf_op | source)
XLA Modules:
  0.0 63.3 jit_solution(4379871894108641926)
XLA Ops:
  0.6 61.6 %decode_step.1 = (f32[2,8,256]{2,1,0:T(8,128)S(1)}, f32[64,3144]{1,0:T(8,128)S(1)}, f32[64,1]{1,0:T(8,128)S(1)}, f32[1,64]{1,0:T(1,128)S(1)}) custom-call(s32[64]{0:T(128)} %lens.1, bf16[64,512]{1,0:T(8,128)(2,1)} %hidden_hbm.1, f32[1,128]{1,0:T(1,128)} %constant.2.clone.freq_hbm, bf16[4,8192,256]{2,1,0:T(8,128)(2,1)} %k_hbm.1, bf16[4,8192,256]{2,1,0:T(8,128)(2,1)} %v_hbm.1, ...), custom_call_target="tpu_custom_call" | custom-call | tf_op jit(solution)/shard_map/decode_step/pallas_call | solution.py:451
  62.2 1.1 %finish_step.1 = (bf16[4,256]{1,0:T(4,128)(2,1)}, bf16[4,256]{1,0:T(4,128)(2,1)}, f32[64,3144]{1,0:T(8,128)}, f32[1,64]{1,0:T(1,128)}) custom-call(f32[2,8,256]{2,1,0:T(8,128)S(1)} %get-tuple-element.12.kv, f32[64,3144]{1,0:T(8,128)S(1)} %get-tuple-element.13.z, f32[64,1]{1,0:T(8,128)S(1)} %get-tuple-element.14.ln, f32[1,64]{1,0:T(1,128)S(1)} %get-tuple-element.15.lr), custom_call_target="tpu_custom_call" | custom-call | tf_op jit(solution)/shard_map/finish_step/pallas_call | solution.py:462

commit v4 on v3

--- a/solution.py
+++ b/solution.py
@@ -36,8 +36,8 @@
                 hid, freq, table, ga, gf, kb0, kb1, kb2, kb3, kb4, vbuf, wq, wkv, wgu, wo, wd,
                 st_send, st_recv, qkv, qkv_recv, q_send, q_recv, qs, kns, vns, os_, sbuf, o_send, o_recv,
                 gup, gu_recv, gux, gux_recv, m_all, mdown, bpart, b_recv, s2_send, s2_recv, fbuf,
-                lsend1, lrecv1, hold, xrecv, lsend2, lrecv2, own, lcol, l_send, l_recv,
-                ld_sem, snd_sem, rcv_sem, l1_sem, lx_sem, l2_sem):
+                lsend1, lrecv1, hold, xrecv, drecv, lsend2, lrecv2, own, lcol, l_send, l_recv,
+                ld_sem, snd_sem, rcv_sem, l1_sem, lx_sem, l2_sem, d_sem, x_ok, y_ok):
     rows, wid, seq, hd, ffc, vb, chunks_a, chunks_b, chunks_c = sizes
     yi = lax.axis_index("yax")
     xi = lax.axis_index("xax")
@@ -60,11 +60,21 @@
     load(HID, (hidden_hbm, hid))
     load(GA, (ga_hbm, ga))
     barrier = pltpu.get_barrier_semaphore()
-    for dy in range(4):
-        for dx in range(4):
-            if dy or dx:
-                pl.semaphore_signal(barrier, inc=1,
-                                    device_id={"yax": (yi + dy) % 4, "xax": (xi + dx) % 4}, device_id_type=MESH)
+    odd = xi % 2 == 1
+    even = xi % 2 == 0
+
+    def signal(sem, yy, xx):
+        pl.semaphore_signal(sem, inc=1, device_id={"yax": yy, "xax": xx}, device_id_type=MESH)
+
+    @pl.when(odd)
+    def _():
+        signal(barrier, yi, x2)
+
+    @pl.when(even)
+    def _():
+        signal(barrier, yi, x1)
+        signal(barrier, yi, x3)
+
     load(FREQ, (freq_hbm, freq))
     load(WQ, (wq_hbm, wq))
     load(WKV, (wk_hbm, wkv.at[0]), (wv_hbm, wkv.at[1]))
@@ -99,15 +109,18 @@
     three = pl.ds(0, 3)
     most = pl.ds(0, 15)
 
-    def transpose_keys(j):
-        loaded(KEY + j, kb[j + 1])
+    tq = seq // 1024
+
+    def transpose_keys(j, start, stop):
+        if start == 0:
+            loaded(KEY + j, kb[j + 1])
 
         def one(t, carry):
             at = pl.ds(pl.multiple_of(t * 256, 256), 256)
             kb[j][at] = kb[j + 1][at].T
             return carry
 
-        lax.fori_loop(0, seq // 256, one, 0, unroll=8)
+        lax.fori_loop(start * tq, stop * tq, one, 0, unroll=tq)
 
     loaded(HID, hid)
     loaded(GA, ga)
@@ -119,7 +132,18 @@
     stat = jnp.where(lane == 0, mean_l, m2_l)
     stat_t = jnp.concatenate([stat, stat], axis=0).T[:8]
     st_send[...] = stat_t
-    pl.semaphore_wait(barrier, 15)
+
+    @pl.when(odd)
+    def _():
+        pl.semaphore_wait(barrier, 3)
+        signal(x_ok, yi, x1)
+
+    @pl.when(even)
+    def _():
+        pl.semaphore_wait(x_ok, 1)
+        for yy in ypeers:
+            signal(barrier, yy, xi)
+
     for xx in xpeers:
         send(st_send, st_recv.at[xi], ST, yi, xx)
     perm = one_hot_rows(96, 64, lambda r: jnp.where(
@@ -134,7 +158,7 @@
     angle = posn.astype(F32) * freq[...]
     table[0] = jnp.cos(angle)
     table[1] = jnp.sin(angle)
-    transpose_keys(0)
+    transpose_keys(0, 0, 4)
     recv(st_recv.at[three], ST)
     parts = [stat_t] + [st_recv[xx] for xx in xpeers]
     means = [p[0:1] for p in parts]
@@ -167,8 +191,8 @@
         if i < 2:
             send(gup.at[xx], gu_recv.at[i], GU, yi, x1)
 
-    transpose_keys(1)
-    transpose_keys(2)
+    transpose_keys(1, 0, 4)
+    transpose_keys(2, 0, 2)
     half = hd // 2
     recv(qkv_recv.at[three, q_rows], QP)
 
@@ -186,6 +210,16 @@
     stacked = jnp.concatenate([r0, r1, r2, r3], axis=0)
     s1 = one_hot_rows(64, 64, lambda r: ((r // 4) % 4) * 16 + (r // 16) * 4 + r % 4)
     q_send[...] = dot(s1, stacked).astype(BF16).reshape(4, 16, 128)
+
+    @pl.when(even)
+    def _():
+        pl.semaphore_wait(barrier, 3)
+        signal(y_ok, yi, x1)
+
+    @pl.when(odd)
+    def _():
+        pl.semaphore_wait(y_ok, 1)
+
     for yy in ypeers:
         send(q_send.at[yy], q_recv.at[yi], Q, yy, xi)
     q_recv[yi] = q_send[yi]
@@ -201,7 +235,8 @@
     recv(gu_recv, GU)
     gux[...] = gup[x2] + gu_recv[1]
     send(gux, gux_recv, GUX, yi, x2)
-    transpose_keys(3)
+    transpose_keys(2, 2, 4)
+    transpose_keys(3, 0, 4)
     recv(q_recv.at[three], Q)
     s2 = one_hot_rows(64, 64, lambda r: ((r // 2) % 4) * 16 + (r % 2) * 8 + (r // 32) * 4 + (r // 8) % 4)
     q_all = dot(s2, q_recv[...].reshape(64, 128))
@@ -315,6 +350,12 @@
         prev = None
         for i, (c0, cn) in enumerate(chunks):
             at = (slots, slice(None), pl.ds(c0, cn))
+            if first + i == 0:
+                hold[at] = logit_part(f, x2, c0, cn).reshape(n, 16, cn)
+                send(hold.at[at], xrecv.at[at], LX, yi, x2, lx_sem.at[0])
+                lsend1[at] = logit_part(f, x3, c0, cn).reshape(n, 16, cn)
+                send(lsend1.at[at], drecv, L1, yi, x3, d_sem)
+                continue
             lsend1[at] = logit_part(f, x3, c0, cn).reshape(n, 16, cn)
             send(lsend1.at[at], lrecv1.at[at], L1, yi, x1, l1_sem.at[first + i])
             hold[at] = logit_part(f, x2, c0, cn).reshape(n, 16, cn)
@@ -345,10 +386,14 @@
     for chunks, slots, ds, first in ((chunks_a, slot_a, (0,), 0), (chunks_b, slot_b, (1, 2, 3), na)):
         for i, (c0, cn) in enumerate(chunks):
             recv_chunk(xrecv.at[slots, :, pl.ds(c0, cn)], lx_sem.at[first + i])
+            if first + i == 0:
+                recv_chunk(drecv, d_sem)
             cs = pl.ds(c0, cn)
             for d in ds:
                 row = pl.ds(pl.multiple_of(((yi + d) % 4) * 16, 16), 16)
                 z = own[d, :, cs] + lrecv2[d, :, cs] + xrecv[d, :, cs]
+                if first + i == 0:
+                    z = z + drecv[0]
                 if c0 + cn > vb:
                     z_out[row, c0:vb] = z[:, :vb - c0]
                     z = jnp.where(lax.broadcasted_iota(jnp.int32, (16, cn), 1) < vb - c0, z, -jnp.inf)
@@ -444,9 +489,9 @@
             v((4, rows, ffc), BF16), v((rows, wid), F32), v((4, 16, wid), F32), v((4, 16, wid), F32),
             v((16, 128), F32), v((4, 16, 128), F32), v((4, 16, wid), BF16),
             v((4, 16, vbp), F32), v((4, 16, vbp), F32), v((4, 16, vbp), F32), v((4, 16, vbp), F32),
-            v((4, 16, vbp), F32), v((4, 16, vbp), F32), v((4, 16, vbp), F32), v((4, 16, 128), F32),
+            v((1, 16, chunks_a[0][1]), F32), v((4, 16, vbp), F32), v((4, 16, vbp), F32), v((4, 16, vbp), F32), v((4, 16, 128), F32),
             v((2, 128), F32), v((16, 2, 128), F32),
-            dma((21,)), dma((16,)), dma((13,)), dma((nx,)), dma((nx,)), dma((nc,)),
+            dma((21,)), dma((16,)), dma((13,)), dma((nx,)), dma((nx,)), dma((nc,)), dma(()), pltpu.SemaphoreType.REGULAR, pltpu.SemaphoreType.REGULAR,
         ]
         kv, z, ln, lr = pl.pallas_call(
             functools.partial(step_kernel, sizes),

time: 63.4 us -> 61.7 us (0.973)
  Pallas kernels: 62.6 us -> 60.9 us
    pallas_call x1, Pallas kernels: 61.6 us -> 59.8 us  [local_step(): pl.pallas_call(functools.partial(step_kernel, sizes), name='decode_step',...]
where the time goes in v4:
time: 61.7 us; the launch traced here: 61.5 us
  Pallas kernels  60.9 us (99%)
  between operations  0.64 us (1%)
    pallas_call x1, Pallas kernels, local_step(): pl.pallas_call(functools.partial(step_kernel, sizes), name='decode_step',...  59.8 us

profile of v4, /device:TPU:0, one launch (start us, length us, event | category | flops | bytes accessed | tf_op | source)
XLA Modules:
  0.0 61.5 jit_solution(9346930083785407328)
XLA Ops:
  0.6 59.8 %decode_step.1 = (f32[2,8,256]{2,1,0:T(8,128)S(1)}, f32[64,3144]{1,0:T(8,128)S(1)}, f32[64,1]{1,0:T(8,128)S(1)}, f32[1,64]{1,0:T(1,128)S(1)}) custom-call(s32[64]{0:T(128)} %lens.1, bf16[64,512]{1,0:T(8,128)(2,1)} %hidden_hbm.1, f32[1,128]{1,0:T(1,128)} %constant.2.clone.freq_hbm, bf16[4,8192,256]{2,1,0:T(8,128)(2,1)} %k_hbm.1, bf16[4,8192,256]{2,1,0:T(8,128)(2,1)} %v_hbm.1, ...), custom_call_target="tpu_custom_call" | custom-call | tf_op jit(solution)/shard_map/decode_step/pallas_call | solution.py:496
  60.5 1.1 %finish_step.1 = (bf16[4,256]{1,0:T(4,128)(2,1)}, bf16[4,256]{1,0:T(4,128)(2,1)}, f32[64,3144]{1,0:T(8,128)}, f32[1,64]{1,0:T(1,128)}) custom-call(f32[2,8,256]{2,1,0:T(8,128)S(1)} %get-tuple-element.12.kv, f32[64,3144]{1,0:T(8,128)S(1)} %get-tuple-element.13.z, f32[64,1]{1,0:T(8,128)S(1)} %get-tuple-element.14.ln, f32[1,64]{1,0:T(1,128)S(1)} %get-tuple-element.15.lr), custom_call_target="tpu_custom_call" | custom-call | tf_op jit(solution)/shard_map/finish_step/pallas_call | solution.py:507

commit v5 on v4

--- a/solution.py
+++ b/solution.py
@@ -45,7 +45,7 @@
     x2 = (xi + 2) % 4
     x3 = (x1 + 2) % 4
     me = yi * 4 + xi
-    ypeers = [(yi + d) % 4 for d in (1, 2, 3)]
+    ypeers = [3 * (1 - yi // 2), 2 - yi // 2, yi + 1 - 2 * (yi % 2)]
     xpeers = [x1, x2, x3]
 
     def load(i, *pairs):
@@ -158,7 +158,7 @@
     angle = posn.astype(F32) * freq[...]
     table[0] = jnp.cos(angle)
     table[1] = jnp.sin(angle)
-    transpose_keys(0, 0, 4)
+    transpose_keys(0, 0, 2)
     recv(st_recv.at[three], ST)
     parts = [stat_t] + [st_recv[xx] for xx in xpeers]
     means = [p[0:1] for p in parts]
@@ -191,8 +191,12 @@
         if i < 2:
             send(gup.at[xx], gu_recv.at[i], GU, yi, x1)
 
+    transpose_keys(0, 2, 4)
+    recv(gu_recv, GU)
+    gux[...] = gup[x2] + gu_recv[1]
+    send(gux, gux_recv, GUX, yi, x2)
     transpose_keys(1, 0, 4)
-    transpose_keys(2, 0, 2)
+    transpose_keys(2, 0, 1)
     half = hd // 2
     recv(qkv_recv.at[three, q_rows], QP)
 
@@ -232,18 +236,13 @@
     kv_out[0] = kns[...]
     kv_out[1] = vns[...]
 
-    recv(gu_recv, GU)
-    gux[...] = gup[x2] + gu_recv[1]
-    send(gux, gux_recv, GUX, yi, x2)
-    transpose_keys(2, 2, 4)
+    transpose_keys(2, 1, 4)
     transpose_keys(3, 0, 4)
     recv(q_recv.at[three], Q)
     s2 = one_hot_rows(64, 64, lambda r: ((r // 2) % 4) * 16 + (r % 2) * 8 + (r // 32) * 4 + (r // 8) % 4)
     q_all = dot(s2, q_recv[...].reshape(64, 128))
     qs[...] = jnp.concatenate([q_all[:32], q_all[32:]], axis=1).reshape(4, 8, hd)
 
-    for j in range(4):
-        loaded(VAL + j, vbuf.at[j])
     scale = hd ** -0.5
     pos = lax.broadcasted_iota(jnp.int32, (8, seq), 1)
 
@@ -253,15 +252,16 @@
             at = pl.ds(t * 256, 256)
             sbuf[j % 2, :, at] = dot(qj, kb[j][at])
 
-    def mix(j):
+    def weights(j):
         s_new = jnp.sum(qs[j] * kns[j:j + 1, :], axis=1, keepdims=True) * scale
         s = jnp.where(pos < lens[me * 4 + j], sbuf[j % 2] * scale, -jnp.inf)
         top = jnp.maximum(jnp.max(s, axis=1, keepdims=True), s_new)
         w = jnp.exp(s - top)
         w_new = jnp.exp(s_new - top)
         inv = 1.0 / (jnp.sum(w, axis=1, keepdims=True) + w_new)
-        prob = (w * inv).astype(BF16)
-        p_new = (w_new * inv).astype(BF16).astype(F32)
+        return (w * inv).astype(BF16), (w_new * inv).astype(BF16).astype(F32)
+
+    def mix(j, prob, p_new):
         hs = seq // 2
         acc = dot(prob[:, :hs], vbuf[j, :hs]) + dot(prob[:, hs:], vbuf[j, hs:])
         os_[j] = acc + p_new * vns[j:j + 1, :]
@@ -281,11 +281,12 @@
 
     scores(0)
     scores(1)
-    mix(0)
+    w0 = weights(0)
+    loaded(VAL, vbuf.at[0])
+    loaded(VAL + 1, vbuf.at[1])
+    mix(0, *w0)
     scores(2)
-    mix(1)
-    scores(3)
-    mix(2)
+    mix(1, *weights(1))
     recv(gux_recv, GUX)
     gu = gup[xi] + gu_recv[0] + gux_recv[...]
     gate = gu[0].astype(BF16).astype(F32)
@@ -293,8 +294,13 @@
     m_all[xi] = (gate * jax.nn.sigmoid(gate) * up_val).astype(BF16)
     for xx in (x2, x3, x1):
         send(m_all.at[xi], m_all.at[xi], M, yi, xx)
+    loaded(VAL + 2, vbuf.at[2])
+    scores(3)
+    mix(2, *weights(2))
+    w3 = weights(3)
+    loaded(VAL + 3, vbuf.at[3])
     send_outputs(0, O1)
-    mix(3)
+    mix(3, *w3)
     send_outputs(1, O2)
     for j in range(4):
         voc = pl.ds(j * vb, vb)
@@ -312,7 +318,7 @@
     a_all = dot(s4, o_rows.astype(BF16)).astype(BF16)
     attn = jnp.concatenate([a_all[i * 64:(i + 1) * 64] for i in range(4)], axis=1)
     bpart[...] = (dot(attn, wo[...]) + mdown[...]).reshape(4, 16, wid)
-    for yy in (ypeers[1], ypeers[0], ypeers[2]):
+    for yy in ypeers:
         send(bpart.at[yy], b_recv.at[yi], B, yy, xi)
     res = hid[pl.ds(pl.multiple_of(yi * 16, 16), 16), :].astype(F32)
     recv(b_recv.at[three], B)
@@ -380,6 +386,7 @@
     recv_chunk(lrecv2, l2_sem.at[0]) if len(chunks_c) == 1 else [
         recv_chunk(lrecv2.at[:, :, pl.ds(c0, cn)], l2_sem.at[i]) for i, (c0, cn) in enumerate(chunks_c)]
     tops, totals = {}, {}
+    order = [yi] + ypeers
     for d in range(4):
         tops[d] = jnp.full((16, 1), -jnp.inf, F32)
         totals[d] = jnp.zeros((16, 1), F32)
@@ -390,7 +397,7 @@
                 recv_chunk(drecv, d_sem)
             cs = pl.ds(c0, cn)
             for d in ds:
-                row = pl.ds(pl.multiple_of(((yi + d) % 4) * 16, 16), 16)
+                row = pl.ds(pl.multiple_of(order[d] * 16, 16), 16)
                 z = own[d, :, cs] + lrecv2[d, :, cs] + xrecv[d, :, cs]
                 if first + i == 0:
                     z = z + drecv[0]
@@ -404,7 +411,7 @@
                 tops[d] = m_new
     lane = lax.broadcasted_iota(jnp.int32, (16, 128), 1)
     for d in range(4):
-        lcol[(yi + d) % 4] = jnp.where(lane == 0, tops[d], totals[d])
+        lcol[order[d]] = jnp.where(lane == 0, tops[d], totals[d])
 
     stat = lcol[...].reshape(rows, 128)
     mine = jnp.concatenate([stat, stat], axis=0).T[0:2]
@@ -467,10 +474,11 @@
         vb = embedding.shape[0] // 4
         inv_freq = np.power(ROPE_BASE, -2.0 * np.arange(hd // 2) / hd).astype(np.float32).reshape(1, hd // 2)
         vbp = -(-vb // 128) * 128
-        def cut(step):
-            return [(c, min(step, vbp - c)) for c in range(0, vbp, step)]
-
-        chunks_a, chunks_b, chunks_c = cut(512), cut(512), cut(1024)
+        def cut(step, start=0):
+            return [(c, min(step, vbp - c)) for c in range(start, vbp, step)]
+
+        chunks_a = [(0, 512)] + cut(768, 512)
+        chunks_b, chunks_c = cut(768), cut(1792)
         nx, nc = len(chunks_a) + len(chunks_b), len(chunks_c)
         sizes = (rows, wid, seq, hd, ffc, vb, chunks_a, chunks_b, chunks_c)
         any_spec = pl.BlockSpec(memory_space=pltpu.HBM)

time: 61.7 us -> 60.5 us (0.981)
  Pallas kernels: 60.9 us -> 59.7 us
    pallas_call x1, Pallas kernels: 59.8 us -> 58.6 us  [local_step(): pl.pallas_call(functools.partial(step_kernel, sizes), name='decode_step',...]
where the time goes in v5:
time: 60.5 us; the launch traced here: 60.3 us
  Pallas kernels  59.7 us (99%)
  between operations  0.64 us (1%)
    pallas_call x1, Pallas kernels, local_step(): pl.pallas_call(functools.partial(step_kernel, sizes), name='decode_step',...  58.6 us

profile of v5, /device:TPU:0, one launch (start us, length us, event | category | flops | bytes accessed | tf_op | source)
XLA Modules:
  0.0 60.3 jit_solution(6487929888307620948)
XLA Ops:
  0.6 58.6 %decode_step.1 = (f32[2,8,256]{2,1,0:T(8,128)S(1)}, f32[64,3144]{1,0:T(8,128)S(1)}, f32[64,1]{1,0:T(8,128)S(1)}, f32[1,64]{1,0:T(1,128)S(1)}) custom-call(s32[64]{0:T(128)} %lens.1, bf16[64,512]{1,0:T(8,128)(2,1)} %hidden_hbm.1, f32[1,128]{1,0:T(1,128)} %constant.2.clone.freq_hbm, bf16[4,8192,256]{2,1,0:T(8,128)(2,1)} %k_hbm.1, bf16[4,8192,256]{2,1,0:T(8,128)(2,1)} %v_hbm.1, ...), custom_call_target="tpu_custom_call" | custom-call | tf_op jit(solution)/shard_map/decode_step/pallas_call | solution.py:504
  59.3 1.1 %finish_step.1 = (bf16[4,256]{1,0:T(4,128)(2,1)}, bf16[4,256]{1,0:T(4,128)(2,1)}, f32[64,3144]{1,0:T(8,128)}, f32[1,64]{1,0:T(1,128)}) custom-call(f32[2,8,256]{2,1,0:T(8,128)S(1)} %get-tuple-element.12.kv, f32[64,3144]{1,0:T(8,128)S(1)} %get-tuple-element.13.z, f32[64,1]{1,0:T(8,128)S(1)} %get-tuple-element.14.ln, f32[1,64]{1,0:T(1,128)S(1)} %get-tuple-element.15.lr), custom_call_target="tpu_custom_call" | custom-call | tf_op jit(solution)/shard_map/finish_step/pallas_call | solution.py:515

commit v6 on v5

--- a/solution.py
+++ b/solution.py
@@ -35,7 +35,7 @@
                 kv_out, z_out, ln_out, lr_out,
                 hid, freq, table, ga, gf, kb0, kb1, kb2, kb3, kb4, vbuf, wq, wkv, wgu, wo, wd,
                 st_send, st_recv, qkv, qkv_recv, q_send, q_recv, qs, kns, vns, os_, sbuf, o_send, o_recv,
-                gup, gu_recv, gux, gux_recv, m_all, mdown, bpart, b_recv, s2_send, s2_recv, fbuf,
+                gup, gu_recv, gux, gux_recv, m_all, mdown, resid, bpart, b_recv, s2_send, s2_recv, fbuf,
                 lsend1, lrecv1, hold, xrecv, drecv, lsend2, lrecv2, own, lcol, l_send, l_recv,
                 ld_sem, snd_sem, rcv_sem, l1_sem, lx_sem, l2_sem, d_sem, x_ok, y_ok):
     rows, wid, seq, hd, ffc, vb, chunks_a, chunks_b, chunks_c = sizes
@@ -90,7 +90,7 @@
     load(WO, (wo_hbm, wo))
     load(GF, (gf_hbm, gf))
 
-    ST, QP, KVP, Q, GU, GUX, M, O1, O2, B, S2, FN, LSE, L1, LX, L2 = range(16)
+    ST, QP, KVP, Q, GU, GUX, M, O1, O2, B1, B2, S2, FN, LSE, L1, LX, L2 = range(17)
 
     def send(src, dst, i, yy, xx, rsem=None):
         pltpu.make_async_remote_copy(src_ref=src, dst_ref=dst, send_sem=snd_sem.at[i],
@@ -146,9 +146,10 @@
 
     for xx in xpeers:
         send(st_send, st_recv.at[xi], ST, yi, xx)
-    perm = one_hot_rows(96, 64, lambda r: jnp.where(
-        r % 24 < 16, ((r % 24) // 4) * 16 + (r // 24) * 4 + r % 4,
-        jnp.where(r % 24 < 20, yi * 16 + (r // 24) * 4 + r % 4, -1)))
+    perm = one_hot_rows(160, 64, lambda r: jnp.where(
+        r >= 96, ((r % 32) // 2) * 4 + ((r - 96) // 32) * 2 + r % 2,
+        jnp.where(r % 24 < 16, ((r % 24) // 4) * 16 + (r // 24) * 4 + r % 4,
+                  jnp.where(r % 24 < 20, yi * 16 + (r // 24) * 4 + r % 4, -1))))
     loaded(FREQ, freq)
     prow = lax.broadcasted_iota(jnp.int32, (24, 128), 0)
     posn = jnp.zeros((24, 128), jnp.int32)
@@ -174,8 +175,9 @@
 
     loaded(WQ, wq)
     loaded(WKV, wkv)
-    q_part = dot(n_perm, wq[...])
-    kv_part = jnp.concatenate([dot(n_perm, wkv[0]), dot(n_perm, wkv[1])], axis=1)
+    n_qkv, n_pair = n_perm[:96], n_perm[96:]
+    q_part = dot(n_qkv, wq[...])
+    kv_part = jnp.concatenate([dot(n_qkv, wkv[0]), dot(n_qkv, wkv[1])], axis=1)
     prow = lax.broadcasted_iota(jnp.int32, (96, 2 * hd), 0)
     qkv[...] = jnp.where(prow % 24 < 16, q_part, kv_part).reshape(4, 24, 2 * hd)
     q_rows, kv_rows = pl.ds(0, 16), pl.ds(16, 8)
@@ -186,8 +188,8 @@
 
     for i, xx in enumerate((x1, x3, x2, xi)):
         loaded(WGU + i, wgu.at[xx])
-        gup[xx, 0] = dot(normed, wgu[xx, 0])
-        gup[xx, 1] = dot(normed, wgu[xx, 1])
+        gup[xx, 0] = dot(n_pair, wgu[xx, 0])
+        gup[xx, 1] = dot(n_pair, wgu[xx, 1])
         if i < 2:
             send(gup.at[xx], gu_recv.at[i], GU, yi, x1)
 
@@ -287,6 +289,7 @@
     mix(0, *w0)
     scores(2)
     mix(1, *weights(1))
+    send_outputs(0, O1)
     recv(gux_recv, GUX)
     gu = gup[xi] + gu_recv[0] + gux_recv[...]
     gate = gu[0].astype(BF16).astype(F32)
@@ -299,30 +302,37 @@
     mix(2, *weights(2))
     w3 = weights(3)
     loaded(VAL + 3, vbuf.at[3])
-    send_outputs(0, O1)
     mix(3, *w3)
     send_outputs(1, O2)
     for j in range(4):
         voc = pl.ds(j * vb, vb)
         load(EMB, (emb_hbm.at[voc, pl.ds(0, hd)], vbuf.at[j, pl.ds(0, vb)]),
              (emb_hbm.at[voc, pl.ds(hd, hd)], vbuf.at[j, pl.ds(seq // 2, vb)]))
+    s5 = one_hot_rows(16, 16, lambda r: ((r % 8) // 2) * 4 + (r // 8) * 2 + r % 2)
+    resid[...] = dot(s5, hid[pl.ds(pl.multiple_of(yi * 16, 16), 16), :])
     loaded(WD, wd)
     loaded(WO, wo)
     loaded(GF, gf)
     recv(m_all.at[three], M)
     mdown[...] = sum([dot(m_all[i], wd[pl.ds(i * ffc, ffc)]) for i in range(4)])
-    s4 = one_hot_rows(256, 256, lambda r: ((r // 2) % 2) * 128 + ((r % 64) // 4) * 8 + (r // 64) * 2 + r % 2)
+    s4 = one_hot_rows(128, 128, lambda r: ((r % 32) // 2) * 8 + (r // 32) * 2 + r % 2)
+
+    def products(pair, i):
+        o_rows = jnp.concatenate([o_recv[pair, k].astype(F32) for k in range(16)], axis=0)
+        a_all = dot(s4, o_rows.astype(BF16)).astype(BF16)
+        attn = jnp.concatenate([a_all[k * 32:(k + 1) * 32] for k in range(4)], axis=1)
+        bpart[pair] = (dot(attn, wo[...]) + mdown[pl.ds(pair * 32, 32)]).reshape(4, 8, wid)
+        for yy in ypeers:
+            send(bpart.at[pair, yy], b_recv.at[pair, yi], i, yy, xi)
+
     recv(o_recv.at[0, most], O1)
+    products(0, B1)
     recv(o_recv.at[1, most], O2)
-    o_rows = jnp.concatenate([o_recv[pair, i].astype(F32) for pair in range(2) for i in range(16)], axis=0)
-    a_all = dot(s4, o_rows.astype(BF16)).astype(BF16)
-    attn = jnp.concatenate([a_all[i * 64:(i + 1) * 64] for i in range(4)], axis=1)
-    bpart[...] = (dot(attn, wo[...]) + mdown[...]).reshape(4, 16, wid)
-    for yy in ypeers:
-        send(bpart.at[yy], b_recv.at[yi], B, yy, xi)
-    res = hid[pl.ds(pl.multiple_of(yi * 16, 16), 16), :].astype(F32)
-    recv(b_recv.at[three], B)
-    res = res + ((bpart[yi] + b_recv[ypeers[0]]) + (b_recv[ypeers[1]] + b_recv[ypeers[2]]))
+    products(1, B2)
+    recv(b_recv.at[0, three], B1)
+    recv(b_recv.at[1, three], B2)
+    res = resid[...] + jnp.concatenate([
+        (bpart[p, yi] + b_recv[p, ypeers[0]]) + (b_recv[p, ypeers[1]] + b_recv[p, ypeers[2]]) for p in range(2)], axis=0)
 
     mean_l = jnp.sum(res, axis=1, keepdims=True) * (1.0 / wid)
     dev = res - mean_l
@@ -337,7 +347,8 @@
     mu = (means[0] + means[1] + means[2] + means[3]) * 0.25
     m2 = m2_l + sum([p[:, 64:65] for p in parts]) + wid * sum([(m - mu) * (m - mu) for m in means])
     rstd = lax.rsqrt(m2 * (1.0 / (4 * wid)) + EPS)
-    f_own = ((res - mu) * rstd * gf[...]).astype(BF16)
+    s6 = one_hot_rows(16, 16, lambda r: ((r // 2) % 2) * 8 + (r // 4) * 2 + r % 2)
+    f_own = dot(s6, ((res - mu) * rstd * gf[...]).astype(BF16)).astype(BF16)
     fbuf[yi] = f_own
     for yy in ypeers:
         send(fbuf.at[yi], fbuf.at[yi], FN, yy, xi)
@@ -431,7 +442,8 @@
     sent(m_all.at[three], M)
     sent(o_recv.at[0, most], O1)
     sent(o_recv.at[1, most], O2)
-    sent(bpart.at[three], B)
+    sent(bpart.at[0, three], B1)
+    sent(bpart.at[1, three], B2)
     sent(s2_recv.at[three], S2)
     sent(fbuf.at[three], FN)
     sent(lsend1, L1)
@@ -494,12 +506,12 @@
             v((4, 16, 128), BF16), v((4, 16, 128), BF16), v((4, 8, hd), F32), v((8, hd), F32), v((8, hd), F32),
             v((4, 8, hd), F32), v((2, 8, seq), F32), v((2, 4, 8, 128), BF16), v((2, 16, 8, 128), BF16),
             v((4, 2, rows, ffc), F32), v((2, 2, rows, ffc), F32), v((2, rows, ffc), F32), v((2, rows, ffc), F32),
-            v((4, rows, ffc), BF16), v((rows, wid), F32), v((4, 16, wid), F32), v((4, 16, wid), F32),
+            v((4, rows, ffc), BF16), v((rows, wid), F32), v((16, wid), F32), v((2, 4, 8, wid), F32), v((2, 4, 8, wid), F32),
             v((16, 128), F32), v((4, 16, 128), F32), v((4, 16, wid), BF16),
             v((4, 16, vbp), F32), v((4, 16, vbp), F32), v((4, 16, vbp), F32), v((4, 16, vbp), F32),
             v((1, 16, chunks_a[0][1]), F32), v((4, 16, vbp), F32), v((4, 16, vbp), F32), v((4, 16, vbp), F32), v((4, 16, 128), F32),
             v((2, 128), F32), v((16, 2, 128), F32),
-            dma((21,)), dma((16,)), dma((13,)), dma((nx,)), dma((nx,)), dma((nc,)), dma(()), pltpu.SemaphoreType.REGULAR, pltpu.SemaphoreType.REGULAR,
+            dma((21,)), dma((17,)), dma((14,)), dma((nx,)), dma((nx,)), dma((nc,)), dma(()), pltpu.SemaphoreType.REGULAR, pltpu.SemaphoreType.REGULAR,
         ]
         kv, z, ln, lr = pl.pallas_call(
             functools.partial(step_kernel, sizes),

time: 60.5 us -> 59.5 us (0.983)
  Pallas kernels: 59.7 us -> 58.7 us
    pallas_call x1, Pallas kernels: 58.6 us -> 57.7 us  [local_step(): pl.pallas_call(functools.partial(step_kernel, sizes), name='decode_step',...]
where the time goes in v6:
time: 59.5 us; the launch traced here: 59.4 us
  Pallas kernels  58.7 us (99%)
  between operations  0.64 us (1%)
    pallas_call x1, Pallas kernels, local_step(): pl.pallas_call(functools.partial(step_kernel, sizes), name='decode_step',...  57.7 us

profile of v6, /device:TPU:0, one launch (start us, length us, event | category | flops | bytes accessed | tf_op | source)
XLA Modules:
  0.0 59.4 jit_solution(15556301008314897522)
XLA Ops:
  0.6 57.7 %decode_step.1 = (f32[2,8,256]{2,1,0:T(8,128)S(1)}, f32[64,3144]{1,0:T(8,128)S(1)}, f32[64,1]{1,0:T(8,128)S(1)}, f32[1,64]{1,0:T(1,128)S(1)}) custom-call(s32[64]{0:T(128)} %lens.1, bf16[64,512]{1,0:T(8,128)(2,1)} %hidden_hbm.1, f32[1,128]{1,0:T(1,128)} %constant.2.clone.freq_hbm, bf16[4,8192,256]{2,1,0:T(8,128)(2,1)} %k_hbm.1, bf16[4,8192,256]{2,1,0:T(8,128)(2,1)} %v_hbm.1, ...), custom_call_target="tpu_custom_call" | custom-call | tf_op jit(solution)/shard_map/decode_step/pallas_call | solution.py:516
  58.3 1.1 %finish_step.1 = (bf16[4,256]{1,0:T(4,128)(2,1)}, bf16[4,256]{1,0:T(4,128)(2,1)}, f32[64,3144]{1,0:T(8,128)}, f32[1,64]{1,0:T(1,128)}) custom-call(f32[2,8,256]{2,1,0:T(8,128)S(1)} %get-tuple-element.12.kv, f32[64,3144]{1,0:T(8,128)S(1)} %get-tuple-element.13.z, f32[64,1]{1,0:T(8,128)S(1)} %get-tuple-element.14.ln, f32[1,64]{1,0:T(1,128)S(1)} %get-tuple-element.15.lr), custom_call_target="tpu_custom_call" | custom-call | tf_op jit(solution)/shard_map/finish_step/pallas_call | solution.py:527

commit v7 on v6

--- a/solution.py
+++ b/solution.py
@@ -33,10 +33,10 @@
                 lens, hidden_hbm, freq_hbm, k_hbm, v_hbm, ga_hbm, wq_hbm, wk_hbm, wv_hbm, wg_hbm, wu_hbm,
                 wo_hbm, wd_hbm, gf_hbm, emb_hbm,
                 kv_out, z_out, ln_out, lr_out,
-                hid, freq, table, ga, gf, kb0, kb1, kb2, kb3, kb4, vbuf, wq, wkv, wgu, wo, wd,
+                hid, small, table, kb0, kb1, kb2, kb3, kb4, vbuf, wqkv, wgu, wdo,
                 st_send, st_recv, qkv, qkv_recv, q_send, q_recv, qs, kns, vns, os_, sbuf, o_send, o_recv,
                 gup, gu_recv, gux, gux_recv, m_all, mdown, resid, bpart, b_recv, s2_send, s2_recv, fbuf,
-                lsend1, lrecv1, hold, xrecv, drecv, lsend2, lrecv2, own, lcol, l_send, l_recv,
+                lbuf, lrecv1, xrecv, drecv, lrecv2, own, lcol, l_send, l_recv,
                 ld_sem, snd_sem, rcv_sem, l1_sem, lx_sem, l2_sem, d_sem, x_ok, y_ok):
     rows, wid, seq, hd, ffc, vb, chunks_a, chunks_b, chunks_c = sizes
     yi = lax.axis_index("yax")
@@ -55,10 +55,12 @@
     def loaded(i, dst):
         pltpu.make_async_copy(dst, dst, ld_sem.at[i]).wait()
 
-    HID, GA, FREQ, WQ, WKV, WGU, WD, WO, GF, KEY, VAL, EMB = 0, 1, 2, 3, 4, 5, 9, 10, 11, 12, 16, 20
+    HID, SMALL, WQKV, WGU, WDO, KEY0, KEY1, KEY2, VAL0, VAL2, VAL3, EMB = range(12)
+    ga, freq, gf = small.at[:, :wid], small.at[:, wid:wid + hd // 2], small.at[:, wid + hd // 2:]
     kb = (kb0, kb1, kb2, kb3, kb4)
+    wd, wo = wdo.at[:4 * ffc], wdo.at[4 * ffc:]
     load(HID, (hidden_hbm, hid))
-    load(GA, (ga_hbm, ga))
+    load(SMALL, (ga_hbm, ga), (freq_hbm, freq), (gf_hbm, gf))
     barrier = pltpu.get_barrier_semaphore()
     odd = xi % 2 == 1
     even = xi % 2 == 0
@@ -75,25 +77,25 @@
         signal(barrier, yi, x1)
         signal(barrier, yi, x3)
 
-    load(FREQ, (freq_hbm, freq))
-    load(WQ, (wq_hbm, wq))
-    load(WKV, (wk_hbm, wkv.at[0]), (wv_hbm, wkv.at[1]))
-    load(KEY, (k_hbm.at[0], kb[1]))
+    load(WQKV, (wq_hbm, wqkv.at[0]), (wk_hbm, wqkv.at[1, :, :hd]), (wv_hbm, wqkv.at[1, :, hd:]))
+    load(KEY0, (k_hbm.at[0], kb[1]))
     for i, xx in enumerate((x1, x3, x2, xi)):
         cols = pl.ds(pl.multiple_of(xx * ffc, ffc), ffc)
-        load(WGU + i, (wg_hbm.at[:, cols], wgu.at[xx, 0]), (wu_hbm.at[:, cols], wgu.at[xx, 1]))
-    for j in range(1, 4):
-        load(KEY + j, (k_hbm.at[j], kb[j + 1]))
-    for j in range(4):
-        load(VAL + j, (v_hbm.at[j], vbuf.at[j]))
-    load(WD, (wd_hbm, wd))
-    load(WO, (wo_hbm, wo))
-    load(GF, (gf_hbm, gf))
+        load(WGU, (wg_hbm.at[:, cols], wgu.at[xx, 0]), (wu_hbm.at[:, cols], wgu.at[xx, 1]))
+    load(KEY1, (k_hbm.at[1], kb[2]))
+    load(KEY2, (k_hbm.at[2], kb[3]), (k_hbm.at[3], kb[4]))
+    load(VAL0, (v_hbm.at[0], vbuf.at[0]), (v_hbm.at[1], vbuf.at[1]))
+    load(VAL2, (v_hbm.at[2], vbuf.at[2]))
+    load(VAL3, (v_hbm.at[3], vbuf.at[3]))
+    load(WDO, (wd_hbm, wd), (wo_hbm, wo))
 
     ST, QP, KVP, Q, GU, GUX, M, O1, O2, B1, B2, S2, FN, LSE, L1, LX, L2 = range(17)
 
+    snd = {ST: 0, S2: 0, QP: 1, KVP: 1, FN: 1, Q: 2, O1: 2, O2: 2, GU: 3, B1: 3, B2: 3, GUX: 4, LSE: 4, M: 5,
+           L1: 5, LX: 5, L2: 5}
+
     def send(src, dst, i, yy, xx, rsem=None):
-        pltpu.make_async_remote_copy(src_ref=src, dst_ref=dst, send_sem=snd_sem.at[i],
+        pltpu.make_async_remote_copy(src_ref=src, dst_ref=dst, send_sem=snd_sem.at[snd[i]],
                                      recv_sem=rcv_sem.at[i] if rsem is None else rsem,
                                      device_id={"yax": yy, "xax": xx}, device_id_type=MESH).start()
 
@@ -104,7 +106,7 @@
         pltpu.make_async_copy(dst, dst, sem).wait()
 
     def sent(src, i):
-        pltpu.make_async_copy(src, src, snd_sem.at[i]).wait()
+        pltpu.make_async_copy(src, src, snd_sem.at[snd[i]]).wait()
 
     three = pl.ds(0, 3)
     most = pl.ds(0, 15)
@@ -112,8 +114,10 @@
     tq = seq // 1024
 
     def transpose_keys(j, start, stop):
-        if start == 0:
-            loaded(KEY + j, kb[j + 1])
+        if start == 0 and j < 2:
+            loaded((KEY0, KEY1)[j], kb[j + 1])
+        elif start == 0 and j == 2:
+            loaded(KEY2, vbuf.at[pl.ds(0, 2)])
 
         def one(t, carry):
             at = pl.ds(pl.multiple_of(t * 256, 256), 256)
@@ -123,7 +127,7 @@
         lax.fori_loop(start * tq, stop * tq, one, 0, unroll=tq)
 
     loaded(HID, hid)
-    loaded(GA, ga)
+    loaded(SMALL, small)
     h = hid[...].astype(F32)
     mean_l = jnp.sum(h, axis=1, keepdims=True) * (1.0 / wid)
     dev = h - mean_l
@@ -150,7 +154,6 @@
         r >= 96, ((r % 32) // 2) * 4 + ((r - 96) // 32) * 2 + r % 2,
         jnp.where(r % 24 < 16, ((r % 24) // 4) * 16 + (r // 24) * 4 + r % 4,
                   jnp.where(r % 24 < 20, yi * 16 + (r // 24) * 4 + r % 4, -1))))
-    loaded(FREQ, freq)
     prow = lax.broadcasted_iota(jnp.int32, (24, 128), 0)
     posn = jnp.zeros((24, 128), jnp.int32)
     for r in range(20):
@@ -173,11 +176,10 @@
     normed = ((h - mu_c) * rstd_c * ga[...]).astype(BF16)
     n_perm = dot(perm, normed).astype(BF16)
 
-    loaded(WQ, wq)
-    loaded(WKV, wkv)
+    loaded(WQKV, wqkv)
     n_qkv, n_pair = n_perm[:96], n_perm[96:]
-    q_part = dot(n_qkv, wq[...])
-    kv_part = jnp.concatenate([dot(n_qkv, wkv[0]), dot(n_qkv, wkv[1])], axis=1)
+    q_part = dot(n_qkv, wqkv[0])
+    kv_part = dot(n_qkv, wqkv[1])
     prow = lax.broadcasted_iota(jnp.int32, (96, 2 * hd), 0)
     qkv[...] = jnp.where(prow % 24 < 16, q_part, kv_part).reshape(4, 24, 2 * hd)
     q_rows, kv_rows = pl.ds(0, 16), pl.ds(16, 8)
@@ -187,7 +189,8 @@
         send(qkv.at[xx, kv_rows], qkv_recv.at[xi, kv_rows], KVP, yi, xx)
 
     for i, xx in enumerate((x1, x3, x2, xi)):
-        loaded(WGU + i, wgu.at[xx])
+        if i == 0:
+            loaded(WGU, wgu)
         gup[xx, 0] = dot(n_pair, wgu[xx, 0])
         gup[xx, 1] = dot(n_pair, wgu[xx, 1])
         if i < 2:
@@ -270,6 +273,10 @@
 
     s3 = one_hot_rows(32, 32, lambda r: ((r // 2) % 2) * 16 + (r % 2) * 8 + (r // 8) * 2 + (r // 4) % 2)
 
+    sent(q_send.at[three], Q)
+    sent(gu_recv, GU)
+    sent(qkv.at[three], QP)
+
     def send_outputs(pair, i):
         o_bf = os_[2 * pair:2 * pair + 2].reshape(16, hd).astype(BF16)
         o_rows = dot(s3, jnp.concatenate([o_bf[:, :half], o_bf[:, half:]], axis=0))
@@ -284,8 +291,7 @@
     scores(0)
     scores(1)
     w0 = weights(0)
-    loaded(VAL, vbuf.at[0])
-    loaded(VAL + 1, vbuf.at[1])
+    loaded(VAL0, vbuf.at[pl.ds(0, 2)])
     mix(0, *w0)
     scores(2)
     mix(1, *weights(1))
@@ -297,11 +303,11 @@
     m_all[xi] = (gate * jax.nn.sigmoid(gate) * up_val).astype(BF16)
     for xx in (x2, x3, x1):
         send(m_all.at[xi], m_all.at[xi], M, yi, xx)
-    loaded(VAL + 2, vbuf.at[2])
+    loaded(VAL2, vbuf.at[2])
     scores(3)
     mix(2, *weights(2))
     w3 = weights(3)
-    loaded(VAL + 3, vbuf.at[3])
+    loaded(VAL3, vbuf.at[3])
     mix(3, *w3)
     send_outputs(1, O2)
     for j in range(4):
@@ -310,9 +316,7 @@
              (emb_hbm.at[voc, pl.ds(hd, hd)], vbuf.at[j, pl.ds(seq // 2, vb)]))
     s5 = one_hot_rows(16, 16, lambda r: ((r % 8) // 2) * 4 + (r // 8) * 2 + r % 2)
     resid[...] = dot(s5, hid[pl.ds(pl.multiple_of(yi * 16, 16), 16), :])
-    loaded(WD, wd)
-    loaded(WO, wo)
-    loaded(GF, gf)
+    loaded(WDO, wdo)
     recv(m_all.at[three], M)
     mdown[...] = sum([dot(m_all[i], wd[pl.ds(i * ffc, ffc)]) for i in range(4)])
     s4 = one_hot_rows(128, 128, lambda r: ((r % 32) // 2) * 8 + (r // 32) * 2 + r % 2)
@@ -339,6 +343,9 @@
     m2_l = jnp.sum(dev * dev, axis=1, keepdims=True)
     lane = lax.broadcasted_iota(jnp.int32, (16, 128), 1)
     s2_send[...] = jnp.where(lane < 64, mean_l, m2_l)
+    sent(st_recv.at[three], ST)
+    sent(gux, GUX)
+    sent(m_all.at[three], M)
     for xx in xpeers:
         send(s2_send, s2_recv.at[xi], S2, yi, xx)
     recv(s2_recv.at[three], S2)
@@ -354,11 +361,13 @@
         send(fbuf.at[yi], fbuf.at[yi], FN, yy, xi)
     loaded(EMB, vbuf.at[:, pl.ds(0, 2 * vb)])
 
+    lsend1, hold, lsend2 = lbuf.at[0], lbuf.at[1], lbuf.at[2]
+
     def logit_part(f, xx, c0, cn):
         return dot_t(f[:, :hd], vbuf[xx, pl.ds(c0, cn)]) + dot_t(f[:, hd:], vbuf[xx, pl.ds(seq // 2 + c0, cn)])
 
     def cross(i, at):
-        recv_chunk(lrecv1.at[at], l1_sem.at[i])
+        recv_chunk(lrecv1.at[at], l1_sem.at[i - 1])
         hold[at] = hold[at] + lrecv1[at]
         send(hold.at[at], xrecv.at[at], LX, yi, x2, lx_sem.at[i])
 
@@ -374,7 +383,7 @@
                 send(lsend1.at[at], drecv, L1, yi, x3, d_sem)
                 continue
             lsend1[at] = logit_part(f, x3, c0, cn).reshape(n, 16, cn)
-            send(lsend1.at[at], lrecv1.at[at], L1, yi, x1, l1_sem.at[first + i])
+            send(lsend1.at[at], lrecv1.at[at], L1, yi, x1, l1_sem.at[first + i - 1])
             hold[at] = logit_part(f, x2, c0, cn).reshape(n, 16, cn)
             if prev is not None:
                 cross(*prev)
@@ -433,22 +442,11 @@
     for xx in xpeers:
         send(l_send, l_recv.at[me], LSE, yi, xx)
     l_recv[me] = mine
-    sent(st_recv.at[three], ST)
-    sent(qkv.at[three, q_rows], QP)
-    sent(qkv.at[three, kv_rows], KVP)
-    sent(q_send.at[three], Q)
-    sent(gu_recv, GU)
-    sent(gux, GUX)
-    sent(m_all.at[three], M)
-    sent(o_recv.at[0, most], O1)
-    sent(o_recv.at[1, most], O2)
-    sent(bpart.at[0, three], B1)
-    sent(bpart.at[1, three], B2)
     sent(s2_recv.at[three], S2)
     sent(fbuf.at[three], FN)
-    sent(lsend1, L1)
-    sent(hold, LX)
-    sent(lsend2, L2)
+    sent(o_recv.at[:, most], O1)
+    sent(bpart.at[:, three], B1)
+    sent(lbuf, L1)
     recv(l_recv.at[most], LSE)
     tops = [l_recv[i, 0:1, :] for i in range(16)]
     top = functools.reduce(jnp.maximum, tops)
@@ -490,7 +488,7 @@
             return [(c, min(step, vbp - c)) for c in range(start, vbp, step)]
 
         chunks_a = [(0, 512)] + cut(768, 512)
-        chunks_b, chunks_c = cut(768), cut(1792)
+        chunks_b, chunks_c = cut(768), [(0, vbp)]
         nx, nc = len(chunks_a) + len(chunks_b), len(chunks_c)
         sizes = (rows, wid, seq, hd, ffc, vb, chunks_a, chunks_b, chunks_c)
         any_spec = pl.BlockSpec(memory_space=pltpu.HBM)
@@ -498,20 +496,20 @@
         v = pltpu.VMEM
         dma = pltpu.SemaphoreType.DMA
         scratch = [
-            v((rows, wid), BF16), v((1, hd // 2), F32), v((2, 24, hd // 2), F32), v((1, wid), F32), v((1, wid), F32),
+            v((rows, wid), BF16), v((1, 2 * wid + hd // 2), F32), v((2, 24, hd // 2), F32),
             *[v((seq, hd), BF16)] * 5, v((4, seq, hd), BF16),
-            v((wid, 2 * hd), BF16), v((2, wid, hd), BF16), v((4, 2, wid, ffc), BF16),
-            v((2 * hd, wid), BF16), v((4 * ffc, wid), BF16),
+            v((2, wid, 2 * hd), BF16), v((4, 2, wid, ffc), BF16),
+            v((4 * ffc + 2 * hd, wid), BF16),
             v((8, 128), F32), v((4, 8, 128), F32), v((4, 24, 2 * hd), F32), v((4, 24, 2 * hd), F32),
             v((4, 16, 128), BF16), v((4, 16, 128), BF16), v((4, 8, hd), F32), v((8, hd), F32), v((8, hd), F32),
             v((4, 8, hd), F32), v((2, 8, seq), F32), v((2, 4, 8, 128), BF16), v((2, 16, 8, 128), BF16),
             v((4, 2, rows, ffc), F32), v((2, 2, rows, ffc), F32), v((2, rows, ffc), F32), v((2, rows, ffc), F32),
             v((4, rows, ffc), BF16), v((rows, wid), F32), v((16, wid), F32), v((2, 4, 8, wid), F32), v((2, 4, 8, wid), F32),
             v((16, 128), F32), v((4, 16, 128), F32), v((4, 16, wid), BF16),
-            v((4, 16, vbp), F32), v((4, 16, vbp), F32), v((4, 16, vbp), F32), v((4, 16, vbp), F32),
-            v((1, 16, chunks_a[0][1]), F32), v((4, 16, vbp), F32), v((4, 16, vbp), F32), v((4, 16, vbp), F32), v((4, 16, 128), F32),
+            v((3, 4, 16, vbp), F32), v((4, 16, vbp), F32), v((4, 16, vbp), F32), v((1, 16, chunks_a[0][1]), F32),
+            v((4, 16, vbp), F32), v((4, 16, vbp), F32), v((4, 16, 128), F32),
             v((2, 128), F32), v((16, 2, 128), F32),
-            dma((21,)), dma((17,)), dma((14,)), dma((nx,)), dma((nx,)), dma((nc,)), dma(()), pltpu.SemaphoreType.REGULAR, pltpu.SemaphoreType.REGULAR,
+            dma((12,)), dma((6,)), dma((14,)), dma((nx - 1,)), dma((nx,)), dma((nc,)), dma(()), pltpu.SemaphoreType.REGULAR, pltpu.SemaphoreType.REGULAR,
         ]
         kv, z, ln, lr = pl.pallas_call(
             functools.partial(step_kernel, sizes),

time: 59.5 us -> 59.3 us (level)
  no operation moved by 1% of the time
where the time goes in v7:
time: 59.3 us; the launch traced here: 59.2 us
  Pallas kernels  58.5 us (99%)
  between operations  0.64 us (1%)
    pallas_call x1, Pallas kernels, local_step(): pl.pallas_call(functools.partial(step_kernel, sizes), name='decode_step',...  57.5 us

profile of v7, /device:TPU:0, one launch (start us, length us, event | category | flops | bytes accessed | tf_op | source)
XLA Modules:
  0.0 59.2 jit_solution(2088359393436179072)
XLA Ops:
  0.6 57.5 %decode_step.1 = (f32[2,8,256]{2,1,0:T(8,128)S(1)}, f32[64,3144]{1,0:T(8,128)S(1)}, f32[64,1]{1,0:T(8,128)S(1)}, f32[1,64]{1,0:T(1,128)S(1)}) custom-call(s32[64]{0:T(128)} %lens.1, bf16[64,512]{1,0:T(8,128)(2,1)} %hidden_hbm.1, f32[1,128]{1,0:T(1,128)} %constant.2.clone.freq_hbm, bf16[4,8192,256]{2,1,0:T(8,128)(2,1)} %k_hbm.1, bf16[4,8192,256]{2,1,0:T(8,128)(2,1)} %v_hbm.1, ...), custom_call_target="tpu_custom_call" | custom-call | tf_op jit(solution)/shard_map/decode_step/pallas_call | solution.py:514
  58.1 1.1 %finish_step.1 = (bf16[4,256]{1,0:T(4,128)(2,1)}, bf16[4,256]{1,0:T(4,128)(2,1)}, f32[64,3144]{1,0:T(8,128)}, f32[1,64]{1,0:T(1,128)}) custom-call(f32[2,8,256]{2,1,0:T(8,128)S(1)} %get-tuple-element.12.kv, f32[64,3144]{1,0:T(8,128)S(1)} %get-tuple-element.13.z, f32[64,1]{1,0:T(8,128)S(1)} %get-tuple-element.14.ln, f32[1,64]{1,0:T(1,128)S(1)} %get-tuple-element.15.lr), custom_call_target="tpu_custom_call" | custom-call | tf_op jit(solution)/shard_map/finish_step/pallas_call | solution.py:525

commit v8 on v7

--- a/solution.py
+++ b/solution.py
@@ -304,10 +304,10 @@
     for xx in (x2, x3, x1):
         send(m_all.at[xi], m_all.at[xi], M, yi, xx)
     loaded(VAL2, vbuf.at[2])
+    loaded(VAL3, vbuf.at[3])
     scores(3)
     mix(2, *weights(2))
     w3 = weights(3)
-    loaded(VAL3, vbuf.at[3])
     mix(3, *w3)
     send_outputs(1, O2)
     for j in range(4):

time: 59.3 us -> 59.2 us (level)
  no operation moved by 1% of the time
where the time goes in v8:
time: 59.2 us; the launch traced here: 59.1 us
  Pallas kernels  58.4 us (99%)
  between operations  0.64 us (1%)
    pallas_call x1, Pallas kernels, local_step(): pl.pallas_call(functools.partial(step_kernel, sizes), name='decode_step',...  57.4 us

profile of v8, /device:TPU:0, one launch (start us, length us, event | category | flops | bytes accessed | tf_op | source)
XLA Modules:
  0.0 59.1 jit_solution(9109384948065198980)
XLA Ops:
  0.6 57.4 %decode_step.1 = (f32[2,8,256]{2,1,0:T(8,128)S(1)}, f32[64,3144]{1,0:T(8,128)S(1)}, f32[64,1]{1,0:T(8,128)S(1)}, f32[1,64]{1,0:T(1,128)S(1)}) custom-call(s32[64]{0:T(128)} %lens.1, bf16[64,512]{1,0:T(8,128)(2,1)} %hidden_hbm.1, f32[1,128]{1,0:T(1,128)} %constant.2.clone.freq_hbm, bf16[4,8192,256]{2,1,0:T(8,128)(2,1)} %k_hbm.1, bf16[4,8192,256]{2,1,0:T(8,128)(2,1)} %v_hbm.1, ...), custom_call_target="tpu_custom_call" | custom-call | tf_op jit(solution)/shard_map/decode_step/pallas_call | solution.py:514
  58.0 1.1 %finish_step.1 = (bf16[4,256]{1,0:T(4,128)(2,1)}, bf16[4,256]{1,0:T(4,128)(2,1)}, f32[64,3144]{1,0:T(8,128)}, f32[1,64]{1,0:T(1,128)}) custom-call(f32[2,8,256]{2,1,0:T(8,128)S(1)} %get-tuple-element.12.kv, f32[64,3144]{1,0:T(8,128)S(1)} %get-tuple-element.13.z, f32[64,1]{1,0:T(8,128)S(1)} %get-tuple-element.14.ln, f32[1,64]{1,0:T(1,128)S(1)} %get-tuple-element.15.lr), custom_call_target="tpu_custom_call" | custom-call | tf_op jit(solution)/shard_map/finish_step/pallas_call | solution.py:525
